TPU v7x, 32 devices: a whole 2x2x4 slice. The times are simulated.
32 devices in a mesh: rep: 4 (over x, y), ep: 8 (over z, core).
Axes of the slice: x: 2, y: 2, z: 4, core: 2. Of those that a mesh axis runs over, the one named last changes fastest.
Arguments:
- x: bfloat16 [1024, 2048], P(('rep', 'ep')), parts along dimension 0
- cache: bfloat16 [1024, 256, 576], P(('rep', 'ep')), parts along dimension 0
- lens: int32 [1024], P(('rep', 'ep')), parts along dimension 0
- ids: int32 [1024, 6], P(('rep', 'ep')), parts along dimension 0
- rw: float32 [1024, 6], P(('rep', 'ep')), parts along dimension 0
- w_q: bfloat16 [2048, 3072], replicated
- w_dkv: bfloat16 [2048, 576], replicated
- w_uk: bfloat16 [16, 128, 512], replicated
- w_uv: bfloat16 [16, 512, 128], replicated
- w_o: bfloat16 [2048, 2048], replicated
- s_gate: bfloat16 [2048, 2816], replicated
- s_up: bfloat16 [2048, 2816], replicated
- s_down: bfloat16 [2816, 2048], replicated
- e_gate: bfloat16 [64, 2048, 1408], P('ep')
- e_up: bfloat16 [64, 2048, 1408], P('ep')
- e_down: bfloat16 [64, 1408, 2048], P('ep')
Outputs:
- output 1: bfloat16 [1024, 2048], P(('rep', 'ep')), parts along dimension 0
- output 2: bfloat16 [1024, 576], P(('rep', 'ep')), parts along dimension 0
There are 4 independent parts. A program takes and returns all parts, laid end to end along the dimension named above; an argument that names none is the same for every part.
All inputs are finite; a program needn't handle non-finite values.
Results may differ from a plain program's by a relative error of at most 0.0119281.
Values are sent between devices in bfloat16 or wider.
A program may use at most 1 GiB of HBM per device.

v0:
```python
import jax
import jax.numpy as jnp
from jax import lax
from jax.sharding import PartitionSpec as P, NamedSharding

EPS = 1e-6
ROPE_BASE = 1.0e4
CAP_FACTOR = 2


def rms(v):
    v = v.astype(jnp.float32)
    return v * lax.rsqrt(jnp.mean(v * v, axis=-1, keepdims=True) + EPS)


def rope(v, pos):
    half = v.shape[-1] // 2
    inv = ROPE_BASE ** (-2.0 * jnp.arange(half, dtype=jnp.float32) / v.shape[-1])
    ang = pos.astype(jnp.float32)[..., None] * inv
    cs = jnp.cos(ang)
    sn = jnp.sin(ang)
    v1 = v[..., :half]
    v2 = v[..., half:]
    return jnp.concatenate([v1 * cs - v2 * sn, v2 * cs + v1 * sn], axis=-1)


def swiglu(u, wg, wu, wd):
    g = jnp.dot(u, wg, preferred_element_type=jnp.float32)
    v = jnp.dot(u, wu, preferred_element_type=jnp.float32)
    return jnp.dot((jax.nn.silu(g) * v).astype(jnp.bfloat16), wd, preferred_element_type=jnp.float32)


def route(col, w, n_col, cap):
    bsz, top = col.shape
    hit = (col[:, :, None] == jnp.arange(n_col)[None, None, :]).astype(jnp.bfloat16)
    flat = hit.reshape(bsz * top, n_col)
    idx = jnp.arange(bsz * top)
    low = (idx[:, None] > idx[None, :]).astype(jnp.bfloat16)
    before = jnp.dot(low, flat, preferred_element_type=jnp.float32)
    rank = jnp.sum(before * flat.astype(jnp.float32), axis=1).astype(jnp.int32).reshape(bsz, top)
    at = (rank[:, :, None] == jnp.arange(cap)[None, None, :]).astype(jnp.bfloat16)
    disp = jnp.einsum('bke,bkr->ber', hit, at, preferred_element_type=jnp.float32).astype(jnp.bfloat16).reshape(bsz, n_col * cap)
    w = w.astype(jnp.float32)
    w1 = w.astype(jnp.bfloat16)
    r1 = w - w1.astype(jnp.float32)
    w2 = r1.astype(jnp.bfloat16)
    w3 = (r1 - w2.astype(jnp.float32)).astype(jnp.bfloat16)
    hw = jnp.stack([w1, w2, w3])[:, :, :, None] * hit[None]
    comb = jnp.einsum('jbke,bkr->jber', hw, at, preferred_element_type=jnp.float32).astype(jnp.bfloat16).reshape(-1, n_col * cap)
    return disp, comb


def attention(x, cache, lens, w_q, w_dkv, w_uk, w_uv, w_o):
    bsz = x.shape[0]
    heads, nope, kvl = w_uk.shape
    kvd = cache.shape[2]
    vh = w_uv.shape[2]
    qkd = nope + kvd - kvl
    xn = rms(x).astype(jnp.bfloat16)
    q = jnp.dot(xn, w_q, preferred_element_type=jnp.float32).astype(jnp.bfloat16).reshape(bsz, heads, qkd)
    kv = jnp.dot(xn, w_dkv, preferred_element_type=jnp.float32)
    kv_new = jnp.concatenate([rms(kv[:, :kvl]), rope(kv[:, kvl:], lens)], axis=-1).astype(jnp.bfloat16)
    q_lat = jnp.einsum('bhd,hdc->bhc', q[:, :, :nope], w_uk, preferred_element_type=jnp.float32).astype(jnp.bfloat16)
    q_rot = rope(q[:, :, nope:].astype(jnp.float32), lens[:, None]).astype(jnp.bfloat16)
    qf = jnp.concatenate([q_lat, q_rot], axis=-1)
    scale = qkd ** -0.5
    s = jnp.einsum('bhc,blc->bhl', qf, cache, preferred_element_type=jnp.float32) * scale
    live = jnp.arange(cache.shape[1])[None, None, :] < lens[:, None, None]
    s = jnp.where(live, s, -jnp.inf)
    s_new = jnp.einsum('bhc,bc->bh', qf, kv_new, preferred_element_type=jnp.float32) * scale
    mx = jnp.maximum(jnp.max(s, axis=2), s_new)
    e = jnp.exp(s - mx[:, :, None])
    e_new = jnp.exp(s_new - mx)
    den = jnp.sum(e, axis=2) + e_new
    p = (e / den[:, :, None]).astype(jnp.bfloat16)
    p_new = (e_new / den).astype(jnp.bfloat16)
    o_all = jnp.einsum('bhl,blc->bhc', p, cache, preferred_element_type=jnp.float32)
    o_lat = (o_all[:, :, :kvl] + p_new.astype(jnp.float32)[:, :, None] * kv_new[:, None, :kvl].astype(jnp.float32)).astype(jnp.bfloat16)
    o = jnp.einsum('bhc,hcv->bhv', o_lat, w_uv, preferred_element_type=jnp.float32).astype(jnp.bfloat16).reshape(bsz, heads * vh)
    a = jnp.dot(o, w_o, preferred_element_type=jnp.float32)
    return (x.astype(jnp.float32) + a).astype(jnp.bfloat16), kv_new


def solution(mesh):
    n = mesh.shape['ep']
    tok_spec = P(('rep', 'ep'))
    row_spec = P(('rep', 'ep'), None)
    cache_spec = P(('rep', 'ep'), None, None)
    exp_spec = P('ep', None, None)

    def local(x, cache, lens, ids, rw, w_q, w_dkv, w_uk, w_uv, w_o, s_gate, s_up, s_down, e_gate, e_up, e_down):
        h1, kv_new = attention(x, cache, lens, w_q, w_dkv, w_uk, w_uv, w_o)
        u = rms(h1).astype(jnp.bfloat16)
        shared = swiglu(u, s_gate, s_up, s_down)
        b_dev, top = ids.shape
        hid = x.shape[1]
        e_loc = e_gate.shape[0]
        n_exp = e_loc * n
        cape = (CAP_FACTOR * b_dev * top + n_exp - 1) // n_exp
        disp, comb = route(ids, rw, n_exp, cape)
        send = jnp.einsum('br,bh->rh', disp, u, preferred_element_type=jnp.float32).astype(jnp.bfloat16)
        recv = lax.all_to_all(send, 'ep', 0, 0, tiled=True)
        xr = recv.reshape(n, e_loc, cape, hid).transpose(1, 0, 2, 3).reshape(e_loc, n * cape, hid)
        g = jnp.einsum('erh,ehi->eri', xr, e_gate, preferred_element_type=jnp.float32)
        v = jnp.einsum('erh,ehi->eri', xr, e_up, preferred_element_type=jnp.float32)
        act = (jax.nn.silu(g) * v).astype(jnp.bfloat16)
        out = jnp.einsum('eri,eih->erh', act, e_down, preferred_element_type=jnp.float32).astype(jnp.bfloat16)
        back = out.reshape(e_loc, n, cape, hid).transpose(1, 0, 2, 3).reshape(n_exp * cape, hid)
        ret = lax.all_to_all(back, 'ep', 0, 0, tiled=True)
        routed = jnp.dot(comb, ret, preferred_element_type=jnp.float32).reshape(-1, b_dev, hid).sum(axis=0)
        y = (h1.astype(jnp.float32) + shared + routed).astype(jnp.bfloat16)
        return y, kv_new

    in_specs = (row_spec, cache_spec, tok_spec, row_spec, row_spec) + (P(),) * 8 + (exp_spec,) * 3
    return jax.shard_map(local, mesh=mesh, in_specs=in_specs, out_specs=(row_spec, row_spec), check_vma=False)
```

profile of v0, /device:TPU:0, one launch (start us, length us, event | category | flops | bytes accessed | tf_op | source)
XLA Modules:
  0.0 187.4 jit_solution(15841547365241628049)
XLA Ops:
  0.6 0.0 copy-start
  0.7 1.2 fusion.32
  1.9 0.0 copy-start.7
  1.9 0.0 copy-start.3
  1.9 7.0 %convolution_convert_fusion = bf16[32,3072]{1,0:T(8,128)(2,1)S(1)} fusion(bf16[2048,3072]{1,0:T(8,128)(2,1)} %param.21, bf16[32,2048]{1,0:T(8,128)(2,1)} %param.16, f32[32]{0:T(128)S(1)} %add_rsqrt_fusion.2), kind=kOutput, calls=%fused_computation.4 | convolution fusion | flops 402948096 | bytes 12910720 | tf_op jit(solution)/shard_map/dot_general | solution.py:60
  8.9 0.3 reshape.166
  9.2 0.0 copy-done.7
  9.3 0.1 iota_compare_fusion.8
  9.3 0.0 copy-done
  9.3 0.0 copy-done.3
  9.4 0.0 copy-start.2
  9.4 0.8 fusion.51
  10.2 0.1 multiply_reduce_fusion.1
  10.3 0.1 fusion.62
  10.4 0.1 subtract_convert_fusion.1
  10.6 2.5 %fusion.17 = bf16[32,16,512]{2,0,1:T(8,128)(2,1)S(1)} fusion(bf16[16,128,512]{2,1,0:T(8,128)(2,1)} %param.23, bf16[32,16,128]{2,1,0:T(8,128)(2,1)S(1)} %slice.40), kind=kOutput, calls=%fused_computation.21 | convolution fusion | flops 67371008 | bytes 2752512 | tf_op jit(solution)/shard_map/bhd,hdc->bhc/dot_general | solution.py:63
  13.1 0.1 subtract_convert_fusion
  13.2 0.1 pad_maximum_fusion
  13.3 0.1 fusion.80
  13.4 0.0 slice-start
  13.4 0.4 fusion.22
  13.8 0.0 copy-done.2
  13.8 1.6 fusion.63
  15.4 0.3 fusion.26
  15.7 0.0 copy-start.4
  15.7 2.4 %fusion.14 = bf16[32,16,512]{2,1,0:T(8,128)(2,1)S(1)} fusion(bf16[32,256,576]{1,2,0:T(8,128)(2,1)S(1)} %copy-done.2, f32[32,512]{1,0:T(8,128)S(1)} %get-tuple-element.2, f32[32,16]{1,0:T(8,128)S(1)} %get-tuple-element.9, f32[32,16,256]{2,1,0:T(8,128)S(1)} %get-tuple-element.16, f32[32,16]{1,0:T(8,128)S(1)} %get-tuple-element.8, ...), kind=kOutput, calls=%fused_computation.19 | convolution fusion | flops 135397376 | bytes 9551872 | tf_op jit(solution)/shard_map/bhl,blc->bhc/dot_general | solution.py:77
  18.1 0.0 copy-done.4
  18.1 0.6 fusion.20
  18.7 0.0 slice-done
  18.7 0.0 slice-done.1
  18.8 0.0 copy-start.5
  18.8 1.7 multiply_reduce_fusion
  20.4 0.0 copy-done.5
  20.5 0.1 copy.47
  20.5 0.1 eq.40
  20.7 0.2 fusion.21
  20.9 0.1 convert_element_type.143
  21.0 0.2 convolution_convert_fusion.6
  21.2 0.1 copy.51
  21.4 0.1 reshape.168
  21.4 0.6 convolution_convert_fusion.1
  22.0 44.1 %all_to_all.21 = bf16[8,48,2048]{2,1,0:T(8,128)(2,1)S(1)} all-to-all(bf16[8,48,2048]{2,1,0:T(8,128)(2,1)S(1)} %bitcast.64), channel_id=1, replica_groups=mesh['rep'=4,'ep'=8] {'ep'}, dimensions={0} | all-to-all | bytes 3145728 | tf_op jit(solution)/shard_map/all_to_all | solution.py:102
  66.1 0.9 copy.52
  67.0 0.9 copy.53
  67.8 19.7 %fusion.9 = f32[8,48,1408]{2,1,0:T(8,128)} fusion(bf16[8,2048,1408]{2,1,0:T(8,128)(2,1)} %param.29, bf16[8,48,2048]{2,0,1:T(8,128)(2,1)S(1)} %bitcast.61), kind=kOutput, calls=%fused_computation.16 | convolution fusion | flops 2214592512 | bytes 49872896 | tf_op jit(solution)/shard_map/erh,ehi->eri/dot_general | solution.py:104
  87.5 20.6 %fusion.3 = bf16[8,48,1408]{2,1,0:T(8,128)(2,1)} fusion(bf16[8,2048,1408]{2,1,0:T(8,128)(2,1)} %param.30, f32[8,48,1408]{2,1,0:T(8,128)} %fusion.9, bf16[8,48,2048]{2,0,1:T(8,128)(2,1)S(1)} %bitcast.62), kind=kOutput, calls=%fused_computation.7 | convolution fusion | flops 2217836544 | bytes 50954240 | tf_op jit(solution)/shard_map/erh,ehi->eri/dot_general | solution.py:105
  108.1 19.9 %convolution_convert_fusion.2 = bf16[8,48,2048]{2,1,0:T(8,128)(2,1)} fusion(bf16[8,48,1408]{2,1,0:T(8,128)(2,1)} %fusion.3, bf16[8,1408,2048]{2,1,0:T(8,128)(2,1)} %param.31), kind=kOutput, calls=%fused_computation.8 | convolution fusion | flops 2215378944 | bytes 48791552 | tf_op jit(solution)/shard_map/eri,eih->erh/dot_general | solution.py:107
  128.0 2.3 %copy.56 = bf16[8,48,2048]{2,0,1:T(8,128)(2,1)S(1)} copy(bf16[8,48,2048]{2,1,0:T(8,128)(2,1)} %convolution_convert_fusion.2) | data formatting | bytes 3145728 | tf_op jit(solution)/shard_map/convert_element_type | solution.py:107
  130.3 0.9 copy.57
  131.1 2.0 %copy.58 = bf16[8,48,2048]{2,1,0:T(8,128)(2,1)} copy(bf16[8,48,2048]{2,0,1:T(8,128)(2,1)S(1)} %bitcast.67) | data formatting | bytes 3145728 | tf_op jit(solution)/shard_map/all_to_all | solution.py:109
  133.2 3.7 %all-to-all-start.1 = ((bf16[8,48,2048]{2,1,0:T(8,128)(2,1)}), bf16[8,48,2048]{2,1,0:T(8,128)(2,1)S(1)}, u32[]{:S(2)}, u32[]{:S(2)}) async-start(bf16[8,48,2048]{2,1,0:T(8,128)(2,1)} %copy.58), calls=%async_computation.1 | async-start | bytes 3145728 | tf_op jit(solution)/shard_map/all_to_all | solution.py:109
  136.9 0.0 copy-done.6
  136.9 0.1 copy.48
  137.0 0.1 fusion.41
  137.2 0.3 fusion.19
  137.5 0.3 copy.50
  137.7 0.2 dot_general.72
  137.9 0.7 pad_maximum_fusion.1
  138.6 6.4 %fusion.61 = f32[32,2816]{1,0:T(8,128)S(1)} fusion(bf16[2048,2816]{1,0:T(8,128)(2,1)} %param.26, f32[32,2048]{1,0:T(8,128)S(1)} %get-tuple-element.18, f32[32]{0:T(128)S(1)} %add_rsqrt_fusion), kind=kOutput, calls=%fused_computation.101 | convolution fusion | flops 369229824 | bytes 12157056 | tf_op jit(solution)/shard_map/dot_general | solution.py:28
  145.0 29.4 %all-to-all-done.1 = bf16[8,48,2048]{2,1,0:T(8,128)(2,1)S(1)} async-done(((bf16[8,48,2048]{2,1,0:T(8,128)(2,1)}), bf16[8,48,2048]{2,1,0:T(8,128)(2,1)S(1)}, u32[]{:S(2)}, u32[]{:S(2)}) %all-to-all-start.1) | async-done | bytes 1572896 | tf_op jit(solution)/shard_map/all_to_all | solution.py:109
  174.4 0.4 convolution_reduce_fusion
  174.9 0.0 copy-start.1
  174.9 12.5 %fusion.5 = bf16[32,2048]{1,0:T(8,128)(2,1)} fusion(f32[32,2048]{1,0:T(8,128)S(1)} %convolution_reduce_fusion, f32[32,2048]{1,0:T(8,128)S(1)} %get-tuple-element.18, bf16[2816,2048]{1,0:T(8,128)(2,1)} %param.28, bf16[2048,2816]{1,0:T(8,128)(2,1)} %param.27, f32[32,2816]{1,0:T(8,128)S(1)} %fusion.61, f32[32]{0:T(128)S(1)} %add_rsqrt_fusion), kind=kOutput, calls=%fused_computation.12 | convolution fusion | flops 739065856 | bytes 24084608 | tf_op jit(solution)/shard_map/dot_general | solution.py:30
  187.4 0.0 copy-done.1
  (16 shorter events, 0.2 us)
Async XLA Ops:
  0.6 8.7 %copy-start = (bf16[2048,576]{0,1:T(8,128)(2,1)S(1)}, bf16[2048,576]{0,1:T(8,128)(2,1)}, u32[]{:S(2)}) copy-start(bf16[2048,576]{0,1:T(8,128)(2,1)} %param.22) | copy-start | bytes 7077892
  1.9 7.4 %copy-start.7 = (s32[32]{0:T(128)S(1)}, s32[32]{0:T(128)}, u32[]{:S(2)}) copy-start(s32[32]{0:T(128)} %param.18) | copy-start | bytes 388
  1.9 7.5 %copy-start.3 = (bf16[32,2048]{1,0:T(8,128)(2,1)S(1)}, bf16[32,2048]{1,0:T(8,128)(2,1)}, u32[]{:S(2)}) copy-start(bf16[32,2048]{1,0:T(8,128)(2,1)} %param.16) | copy-start | bytes 393220
  9.4 4.4 %copy-start.2 = (bf16[32,256,576]{1,2,0:T(8,128)(2,1)S(1)}, bf16[32,256,576]{1,2,0:T(8,128)(2,1)}, u32[]{:S(2)}) copy-start(bf16[32,256,576]{1,2,0:T(8,128)(2,1)} %param.17) | copy-start | bytes 28311556
  13.4 5.3 %slice-start = ((s8[8388608]{0:T(1024)(128)(4,1)}), s8[4194304]{0:T(1024)(128)(4,1)S(1)}, s32[]{:S(2)}) async-start(s8[8388608]{0:T(1024)(128)(4,1)} %bitcast.59), calls=%async_computation.2 | async-start | bytes 8388608
  13.8 5.0 %slice-start.1 = ((s8[8388608]{0:T(1024)(128)(4,1)}), s8[4194304]{0:T(1024)(128)(4,1)S(1)}, s32[]{:S(2)}) async-start(s8[8388608]{0:T(1024)(128)(4,1)} %bitcast.59), calls=%async_computation.3 | async-start | bytes 8388608
  15.7 2.5 %copy-start.4 = (bf16[16,512,128]{2,1,0:T(8,128)(2,1)S(1)}, bf16[16,512,128]{2,1,0:T(8,128)(2,1)}, u32[]{:S(2)}) copy-start(bf16[16,512,128]{2,1,0:T(8,128)(2,1)} %param.24) | copy-start | bytes 6291460
  18.8 1.7 copy-start.5
  133.2 3.7 %copy-start.6 = (f32[32,6]{0,1:T(8,128)S(1)}, f32[32,6]{0,1:T(8,128)}, u32[]{:S(2)}) copy-start(f32[32,6]{0,1:T(8,128)} %param.20) | copy-start | bytes 2308
  133.2 41.3 %all-to-all-start.1 = ((bf16[8,48,2048]{2,1,0:T(8,128)(2,1)}), bf16[8,48,2048]{2,1,0:T(8,128)(2,1)S(1)}, u32[]{:S(2)}, u32[]{:S(2)}) async-start(bf16[8,48,2048]{2,1,0:T(8,128)(2,1)} %copy.58), calls=%async_computation.1 | async-start | bytes 3145728 | tf_op jit(solution)/shard_map/all_to_all | solution.py:109
  174.9 12.5 %copy-start.1 = (bf16[2048,576]{0,1:T(8,128)(2,1)S(1)}, bf16[2048,576]{0,1:T(8,128)(2,1)}, u32[]{:S(2)}) copy-start(bf16[2048,576]{0,1:T(8,128)(2,1)} %param.22) | copy-start | bytes 7077892
where the time goes:
time: 188 us; the launch traced here: 187 us
  matrix products  97.7 us (52%)
  blocking collectives  44.1 us (23%)
  waiting for transfers between devices  29.4 us (16%)
  local copies, waits for them, and re-layouts  8.39 us (4%)
  starting transfers between devices  3.71 us (2%)
  other arithmetic  3.13 us (2%)
    all_to_all x1, blocking collectives, local(): recv = lax.all_to_all(send, 'ep', 0, 0, tiled=True)  44.1 us
    all_to_all x1, waiting for transfers between devices, local(): ret = lax.all_to_all(back, 'ep', 0, 0, tiled=True)  29.4 us
    dot_general x1, matrix products, local(): v = jnp.einsum('erh,ehi->eri', xr, e_up, preferred_element_type=jnp.float32)  20.6 us
    dot_general x1, matrix products, local(): jnp.einsum('eri,eih->erh', act, e_down, preferred_element_type=jnp.float32)  19.9 us
    dot_general x1, matrix products, local(): jnp.einsum('erh,ehi->eri', xr, e_gate, preferred_element_type=jnp.float32)  19.7 us
    dot_general x1, matrix products, swiglu(): jnp.dot((jax.nn.silu(g) * v).astype(jnp.bfloat16), wd, preferred_element_...  12.5 us
    dot_general x1, matrix products, attention(): jnp.dot(xn, w_q, preferred_element_type=jnp.float32).astype(jnp.bfloat16)  6.97 us
    dot_general x1, matrix products, swiglu(): g = jnp.dot(u, wg, preferred_element_type=jnp.float32)  6.4 us
  transfers between devices with their start and end apart: 1, of which 1 were waited for; matrix products, arithmetic and copies ran while one was open for 4% of the time, Pallas kernels for 0%

commit v1 on v0

v1 whole, which is shorter than its diff:
```python
import functools

import jax
import jax.numpy as jnp
from jax import lax
from jax.experimental import pallas as pl
from jax.experimental.pallas import tpu as pltpu
from jax.sharding import PartitionSpec as P

EPS = 1e-6
ROPE_BASE = 1.0e4
CAP_FACTOR = 2
N_A = 5
N_B = 3
CW = 256
F32 = jnp.float32
BF16 = jnp.bfloat16


def rms(v):
    v = v.astype(jnp.float32)
    return v * lax.rsqrt(jnp.mean(v * v, axis=-1, keepdims=True) + EPS)


def rope(v, pos):
    half = v.shape[-1] // 2
    inv = ROPE_BASE ** (-2.0 * jnp.arange(half, dtype=jnp.float32) / v.shape[-1])
    ang = pos.astype(jnp.float32)[..., None] * inv
    cs = jnp.cos(ang)
    sn = jnp.sin(ang)
    v1 = v[..., :half]
    v2 = v[..., half:]
    return jnp.concatenate([v1 * cs - v2 * sn, v2 * cs + v1 * sn], axis=-1)


def attention(x, cache, lens, w_q, w_dkv, w_uk, w_uv, w_o):
    bsz = x.shape[0]
    heads, nope, kvl = w_uk.shape
    kvd = cache.shape[2]
    vh = w_uv.shape[2]
    qkd = nope + kvd - kvl
    xn = rms(x).astype(jnp.bfloat16)
    q = jnp.dot(xn, w_q, preferred_element_type=jnp.float32).astype(jnp.bfloat16).reshape(bsz, heads, qkd)
    kv = jnp.dot(xn, w_dkv, preferred_element_type=jnp.float32)
    kv_new = jnp.concatenate([rms(kv[:, :kvl]), rope(kv[:, kvl:], lens)], axis=-1).astype(jnp.bfloat16)
    q_lat = jnp.einsum('bhd,hdc->bhc', q[:, :, :nope], w_uk, preferred_element_type=jnp.float32).astype(jnp.bfloat16)
    q_rot = rope(q[:, :, nope:].astype(jnp.float32), lens[:, None]).astype(jnp.bfloat16)
    qf = jnp.concatenate([q_lat, q_rot], axis=-1)
    scale = qkd ** -0.5
    s = jnp.einsum('bhc,blc->bhl', qf, cache, preferred_element_type=jnp.float32) * scale
    live = jnp.arange(cache.shape[1])[None, None, :] < lens[:, None, None]
    s = jnp.where(live, s, -jnp.inf)
    s_new = jnp.einsum('bhc,bc->bh', qf, kv_new, preferred_element_type=jnp.float32) * scale
    mx = jnp.maximum(jnp.max(s, axis=2), s_new)
    e = jnp.exp(s - mx[:, :, None])
    e_new = jnp.exp(s_new - mx)
    den = jnp.sum(e, axis=2) + e_new
    p = (e / den[:, :, None]).astype(jnp.bfloat16)
    p_new = (e_new / den).astype(jnp.bfloat16)
    o_all = jnp.einsum('bhl,blc->bhc', p, cache, preferred_element_type=jnp.float32)
    o_lat = (o_all[:, :, :kvl] + p_new.astype(jnp.float32)[:, :, None] * kv_new[:, None, :kvl].astype(jnp.float32)).astype(jnp.bfloat16)
    o = jnp.einsum('bhc,hcv->bhv', o_lat, w_uv, preferred_element_type=jnp.float32).astype(jnp.bfloat16).reshape(bsz, heads * vh)
    a = jnp.dot(o, w_o, preferred_element_type=jnp.float32)
    return (x.astype(jnp.float32) + a).astype(jnp.bfloat16), kv_new


def moe_kernel(n, cap, u_ref, h1_ref, meta_ref, eg, eu, ed, sg, su, sd, y_ref,
               wa, wb, meta_all, u_all, xr, act, disp, comb_t, comb, rows,
               pown, psend, precv, zsum, zrecv, sact,
               sem_a, sem_b, ms, mr, us, ur, fs, fr, ps, pr, zs, zr):
    me = lax.axis_index('ep')
    nz = n // 2
    zi = me // 2
    co = lax.rem(me, 2)
    mate = zi * 2 + 1 - co
    b_dev, hid = u_ref.shape
    e_loc, _, inter = eg.shape
    slots = e_loc * cap
    n_tok = n * b_dev
    half = nz * b_dev
    n_ch = hid // CW

    def dev(d):
        return {'ep': d}

    def at_z(dz):
        return lax.rem(zi + dz, nz) * 2 + co

    def from_z(dz):
        return lax.rem(zi + nz - dz, nz)

    def a_copy(src, slot):
        return pltpu.make_async_copy(src, wa.at[slot], sem_a.at[slot])

    def start_gu(e, k):
        a_copy(eg.at[e], lax.rem(2 * e, N_A)).start()
        a_copy(eu.at[e], lax.rem(2 * e + 1, N_A)).start()

    def start_down(j):
        slot = lax.rem(j, N_B)
        for e in range(e_loc):
            pltpu.make_async_copy(
                ed.at[e, :, pl.ds(pl.multiple_of(j * CW, CW), CW)],
                wb.at[slot, :, pl.ds(e * CW, CW)], sem_b.at[slot]).start()

    def wait_a(slot):
        a_copy(eg.at[0], slot).wait()

    def wait_b(slot):
        pltpu.make_async_copy(sd.at[pl.ds(0, inter)], wb.at[slot], sem_b.at[slot]).wait()

    n_gu = 2 * e_loc
    sh_a = [(sg, 0), (su, 0), (sg, 1), (su, 1)]

    def start_unit_a(i):
        slot = i % N_A
        if i < n_gu:
            a_copy((eg if i % 2 == 0 else eu).at[i // 2], slot).start()
        else:
            r, h = sh_a[i - n_gu]
            a_copy(r.at[:, pl.ds(h * inter, inter)], slot).start()

    for i in range(N_A):
        start_unit_a(i)
    for j in range(N_B):
        start_down(j)

    barrier = pltpu.get_barrier_semaphore()
    for d in range(1, n):
        pl.semaphore_signal(barrier, inc=1, device_id=dev(lax.rem(me + d, n)))
    pl.semaphore_wait(barrier, n - 1)

    def meta_copy(d):
        return pltpu.make_async_remote_copy(
            meta_ref, meta_all.at[me], ms.at[d - 1], mr.at[d - 1],
            device_id=dev(lax.rem(me + d, n)), device_id_type=pl.DeviceIdType.MESH)

    my_rows = pl.ds(pl.multiple_of(me * b_dev, b_dev), b_dev)

    def u_copy(k, target):
        return pltpu.make_async_remote_copy(
            u_ref, u_all.at[my_rows], us.at[k], ur.at[k],
            device_id=dev(target), device_id_type=pl.DeviceIdType.MESH)

    def fwd_copy(dz):
        blk = from_z(dz) * 2 + co
        r = u_all.at[pl.ds(pl.multiple_of(blk * b_dev, b_dev), b_dev)]
        return pltpu.make_async_remote_copy(
            r, r, fs.at[dz - 1], fr.at[dz - 1],
            device_id=dev(mate), device_id_type=pl.DeviceIdType.MESH)

    def recv_wait(dst, sem):
        pltpu.make_async_remote_copy(
            dst, dst, us.at[0], sem, device_id=dev(mate),
            device_id_type=pl.DeviceIdType.MESH).wait_recv()

    for d in range(1, n):
        meta_copy(d).start()
    for dz in range(1, nz):
        u_copy(dz - 1, at_z(dz)).start()
    u_copy(nz - 1, mate).start()
    u_all[my_rows] = u_ref[...]

    tot = meta_ref[...]
    for d in range(1, n):
        src = lax.rem(me + n - d, n)
        recv_wait(meta_all.at[src], mr.at[d - 1])
        tot = tot + meta_all[src]
    half_m = tot.shape[0] // 2
    lane = lax.broadcasted_iota(jnp.int32, (e_loc, n_tok), 0) + (me * e_loc + 1)
    lane = lane.astype(F32)
    hit = jnp.zeros((e_loc, n_tok), F32)
    wt = jnp.zeros((e_loc, n_tok), F32)
    for k in range(half_m):
        eq = tot[k:k + 1] == lane
        hit = hit + jnp.where(eq, 1.0, 0.0)
        wt = wt + jnp.where(eq, tot[half_m + k:half_m + k + 1], 0.0)
    r0 = lax.broadcasted_iota(jnp.int32, (n_tok, n_tok), 0)
    r1 = lax.broadcasted_iota(jnp.int32, (n_tok, n_tok), 1)
    before = jnp.where(r0 < r1, 1.0, 0.0).astype(BF16)
    rank = jnp.dot(hit.astype(BF16), before, preferred_element_type=F32)
    rank = jnp.where(hit > 0.5, rank, -1.0)
    w1 = wt.astype(BF16).astype(F32)
    rest = wt - w1
    w2 = rest.astype(BF16).astype(F32)
    w3 = rest - w2
    row = lax.broadcasted_iota(jnp.int32, (cap, n_tok), 0).astype(F32)
    for e in range(e_loc):
        m = row == rank[e:e + 1]
        disp[e * cap:(e + 1) * cap] = jnp.where(m, 1.0, 0.0).astype(BF16)
        for p, w in enumerate((w1, w2, w3)):
            comb_t[p * slots + e * cap:p * slots + (e + 1) * cap] = jnp.where(m, w[e:e + 1], 0.0).astype(BF16)
    side = r0 // half
    blk = lax.rem(r0, half) // b_dev
    chip = lax.rem(blk + zi, nz)
    core = jnp.where(side == 0, co, 1 - co)
    tok = (chip * 2 + core) * b_dev + lax.rem(r0, b_dev)
    perm = jnp.where(r1 == tok, 1.0, 0.0).astype(BF16)
    comb[...] = lax.dot_general(perm, comb_t[...], (((1,), (1,)), ((), ())),
                                preferred_element_type=F32).astype(BF16)

    for dz in range(1, nz):
        blk_z = from_z(dz) * 2 + co
        recv_wait(u_all.at[pl.ds(pl.multiple_of(blk_z * b_dev, b_dev), b_dev)], ur.at[dz - 1])
        fwd_copy(dz).start()
    recv_wait(u_all.at[pl.ds(pl.multiple_of(mate * b_dev, b_dev), b_dev)], ur.at[nz - 1])
    for dz in range(1, nz):
        blk_z = from_z(dz) * 2 + 1 - co
        recv_wait(u_all.at[pl.ds(pl.multiple_of(blk_z * b_dev, b_dev), b_dev)], fr.at[dz - 1])

    @pl.loop(0, hid // 512)
    def _(i):
        cols = pl.ds(pl.multiple_of(i * 512, 512), 512)
        xr[:, cols] = jnp.dot(disp[...], u_all[:, cols], preferred_element_type=F32).astype(BF16)

    def gate_up(x, sa, sb, store):
        for c0 in range(0, inter, CW):
            c1 = min(c0 + CW, inter)
            g = jnp.dot(x, wa[sa, :, c0:c1], preferred_element_type=F32)
            v = jnp.dot(x, wa[sb, :, c0:c1], preferred_element_type=F32)
            store(c0, c1, (jax.nn.silu(g) * v).astype(BF16))

    def expert_body(e):
        sa = lax.rem(2 * e, N_A)
        sb = lax.rem(2 * e + 1, N_A)
        wait_a(sa)
        wait_a(sb)
        rs = pl.ds(pl.multiple_of(e * cap, cap), cap)

        def store(c0, c1, val):
            act[rs, c0:c1] = val

        gate_up(xr[rs, :], sa, sb, store)

    @pl.loop(0, e_loc)
    def _(e):
        expert_body(e)
        for t in range(2):
            i = 2 * e + t + N_A
            slot = lax.rem(i, N_A)

            @pl.when(jnp.logical_and(i < n_gu, lax.rem(i, 2) == 0))
            def _():
                a_copy(eg.at[lax.min(i // 2, e_loc - 1)], slot).start()

            @pl.when(jnp.logical_and(i < n_gu, lax.rem(i, 2) == 1))
            def _():
                a_copy(eu.at[lax.min(i // 2, e_loc - 1)], slot).start()

            for q in range(4):
                @pl.when(i == n_gu + q)
                def _():
                    r, h = sh_a[q]
                    a_copy(r.at[:, pl.ds(h * inter, inter)], slot).start()

    def p_copy(j):
        return pltpu.make_async_remote_copy(
            psend.at[j], precv.at[j], ps.at[j], pr.at[j],
            device_id=dev(mate), device_id_type=pl.DeviceIdType.MESH)

    def z_copy(j, dz):
        return pltpu.make_async_remote_copy(
            zsum.at[j, pl.ds(dz * b_dev, b_dev)], zrecv.at[j, dz - 1],
            zs.at[j, dz - 1], zr.at[j, dz - 1],
            device_id=dev(at_z(dz)), device_id_type=pl.DeviceIdType.MESH)

    def pass_on(j):
        recv_wait(precv.at[j], pr.at[j])
        zsum[j] = pown[j] + precv[j]
        for dz in range(1, nz):
            z_copy(j, dz).start()

    @pl.loop(0, n_ch)
    def _(j):
        slot = lax.rem(j, N_B)
        wait_b(slot)
        for e in range(e_loc):
            rows[e * cap:(e + 1) * cap] = jnp.dot(
                act[e * cap:(e + 1) * cap], wb[slot, :, e * CW:(e + 1) * CW],
                preferred_element_type=F32).astype(BF16)

        @pl.when(j + N_B < n_ch)
        def _():
            start_down(lax.min(j + N_B, n_ch - 1))

        for h in range(2):
            i = n_ch + h

            @pl.when(j + N_B == i)
            def _():
                pltpu.make_async_copy(sd.at[pl.ds(h * inter, inter)], wb.at[i % N_B], sem_b.at[i % N_B]).start()

        part = jnp.dot(comb[:, 0:slots], rows[...], preferred_element_type=F32)
        part += jnp.dot(comb[:, slots:2 * slots], rows[...], preferred_element_type=F32)
        part += jnp.dot(comb[:, 2 * slots:3 * slots], rows[...], preferred_element_type=F32)
        pown[j] = part[:half]
        psend[j] = part[half:]
        p_copy(j).start()

        @pl.when(j > 0)
        def _():
            pass_on(lax.max(j - 1, 0))

    for h in range(2):
        sa = (n_gu + 2 * h) % N_A
        sb = (n_gu + 2 * h + 1) % N_A
        wait_a(sa)
        wait_a(sb)

        def store(c0, c1, val):
            sact[:, h * inter + c0:h * inter + c1] = val

        gate_up(u_ref[...], sa, sb, store)
        if h == 0:
            pass_on(n_ch - 1)
    for h in range(2):
        wait_b((n_ch + h) % N_B)

    for j in range(n_ch):
        cols = slice(j * CW, (j + 1) * CW)
        s = jnp.dot(sact[:, :inter], wb[n_ch % N_B, :, cols], preferred_element_type=F32)
        s += jnp.dot(sact[:, inter:], wb[(n_ch + 1) % N_B, :, cols], preferred_element_type=F32)
        routed = zsum[j, :b_dev]
        for dz in range(1, nz):
            recv_wait(zrecv.at[j, dz - 1], zr.at[j, dz - 1])
            routed = routed + zrecv[j, dz - 1]
        y_ref[:, cols] = (h1_ref[:, cols].astype(F32) + s + routed).astype(BF16)

    for d in range(1, n):
        meta_copy(d).wait_send()
    for dz in range(1, nz):
        u_copy(dz - 1, at_z(dz)).wait_send()
        fwd_copy(dz).wait_send()
    u_copy(nz - 1, mate).wait_send()
    for j in range(n_ch):
        p_copy(j).wait_send()
        for dz in range(1, nz):
            z_copy(j, dz).wait_send()


def moe(n, u, h1, meta, eg, eu, ed, sg, su, sd, cap):
    b_dev, hid = u.shape
    e_loc, _, inter = eg.shape
    n_tok = n * b_dev
    slots = e_loc * cap
    nz = n // 2
    half = nz * b_dev
    n_ch = hid // CW
    dma = pltpu.SemaphoreType.DMA
    vm = pl.BlockSpec(memory_space=pltpu.VMEM)
    anys = pl.BlockSpec(memory_space=pl.ANY)
    flops = 2 * 3 * hid * inter * (slots + 2 * b_dev)
    return pl.pallas_call(
        functools.partial(moe_kernel, n, cap),
        out_shape=jax.ShapeDtypeStruct((b_dev, hid), BF16),
        in_specs=[vm, vm, vm] + [anys] * 6,
        out_specs=vm,
        scratch_shapes=[
            pltpu.VMEM((N_A, hid, inter), BF16),
            pltpu.VMEM((N_B, inter, hid), BF16),
            pltpu.VMEM((n,) + meta.shape, F32),
            pltpu.VMEM((n_tok, hid), BF16),
            pltpu.VMEM((slots, hid), BF16),
            pltpu.VMEM((slots, inter), BF16),
            pltpu.VMEM((slots, n_tok), BF16),
            pltpu.VMEM((3 * slots, n_tok), BF16),
            pltpu.VMEM((n_tok, 3 * slots), BF16),
            pltpu.VMEM((slots, CW), BF16),
            pltpu.VMEM((n_ch, half, CW), F32),
            pltpu.VMEM((n_ch, half, CW), F32),
            pltpu.VMEM((n_ch, half, CW), F32),
            pltpu.VMEM((n_ch, half, CW), F32),
            pltpu.VMEM((n_ch, nz - 1, b_dev, CW), F32),
            pltpu.VMEM((b_dev, 2 * inter), BF16),
            dma((N_A,)), dma((N_B,)),
            dma((n - 1,)), dma((n - 1,)),
            dma((nz,)), dma((nz,)),
            dma((nz - 1,)), dma((nz - 1,)),
            dma((n_ch,)), dma((n_ch,)),
            dma((n_ch, nz - 1)), dma((n_ch, nz - 1)),
        ],
        compiler_params=pltpu.CompilerParams(
            collective_id=0, has_side_effects=True, vmem_limit_bytes=63 << 20),
        cost_estimate=pl.CostEstimate(flops=flops, bytes_accessed=30 * hid * inter * 2, transcendentals=0),
        name="moe",
    )(u, h1, meta, eg, eu, ed, sg, su, sd)


def solution(mesh):
    n = mesh.shape['ep']
    tok_spec = P(('rep', 'ep'))
    row_spec = P(('rep', 'ep'), None)
    cache_spec = P(('rep', 'ep'), None, None)
    exp_spec = P('ep', None, None)

    def local(x, cache, lens, ids, rw, w_q, w_dkv, w_uk, w_uv, w_o, s_gate, s_up, s_down, e_gate, e_up, e_down):
        b_dev, top = ids.shape
        e_loc = e_gate.shape[0]
        n_exp = e_loc * n
        cape = (CAP_FACTOR * b_dev * top + n_exp - 1) // n_exp
        me = lax.axis_index('ep')
        here = (jnp.arange(n * b_dev) // b_dev == me)[None]
        pad = ((0, 8 - top), (0, 0))

        def spread(v):
            return jnp.where(here, jnp.tile(jnp.pad(v.T, pad), (1, n)), 0.0)

        meta = jnp.concatenate([spread(ids.astype(F32) + 1.0), spread(rw.astype(F32))], axis=0)
        h1, kv_new = attention(x, cache, lens, w_q, w_dkv, w_uk, w_uv, w_o)
        u = rms(h1).astype(jnp.bfloat16)
        y = moe(n, u, h1, meta, e_gate, e_up, e_down, s_gate, s_up, s_down, n * cape)
        return y, kv_new

    in_specs = (row_spec, cache_spec, tok_spec, row_spec, row_spec) + (P(),) * 8 + (exp_spec,) * 3
    return jax.shard_map(local, mesh=mesh, in_specs=in_specs, out_specs=(row_spec, row_spec), check_vma=False)
```

time: 188 us -> 112 us (0.60)
  Pallas kernels: 0 us -> 74 us
  matrix products: 97.7 us -> 27.4 us
  blocking collectives: 44.1 us -> 0 us
  waiting for transfers between devices: 29.4 us -> 0 us
  local copies, waits for them, and re-layouts: 8.39 us -> 2.87 us
  starting transfers between devices: 3.71 us -> 0 us
  other arithmetic: 3.13 us -> 6.22 us
    dot_general x10 -> x0, matrix products: 80.8 us -> none  [the longest x1 20.6 us: local(): v = jnp.einsum('erh,ehi->eri', xr, e_up, preferred_element_type=jnp.float32)]
    pallas_call x0 -> x1, Pallas kernels: none -> 74 us  [moe(): pl.pallas_call(functools.partial(moe_kernel, n, cap), out_shape=jax.Shape...]
    all_to_all x1 -> x0, blocking collectives: 44.1 us -> none  [local(): recv = lax.all_to_all(send, 'ep', 0, 0, tiled=True)]
    all_to_all x1 -> x0, waiting for transfers between devices: 29.4 us -> none  [local(): ret = lax.all_to_all(back, 'ep', 0, 0, tiled=True)]
    all_to_all x1 -> x0, starting transfers between devices: 3.71 us -> none  [local(): ret = lax.all_to_all(back, 'ep', 0, 0, tiled=True)]
    dot_general x1, matrix products: 1.57 us -> 5.25 us  [attention(): jnp.einsum('bhc,blc->bhl', qf, cache, preferred_element_type=jnp.float32)]
    dot_general x1, matrix products: 2.44 us -> 5.85 us  [attention(): jnp.einsum('bhl,blc->bhc', p, cache, preferred_element_type=jnp.float32)]
    dot_general x1, matrix products: 1.66 us -> 5.04 us  [attention(): a = jnp.dot(o, w_o, preferred_element_type=jnp.float32)]
  transfers between devices with their start and end apart: 1 -> 0, of which waited for: 1 -> 0; matrix products, arithmetic and copies ran while one was open for 4% -> 0% of each run, Pallas kernels for 0% -> 0%
where the time goes in v1:
time: 112 us; the launch traced here: 111 us
  Pallas kernels  74 us (66%)
  matrix products  27.4 us (24%)
  other arithmetic  6.22 us (6%)
  local copies, waits for them, and re-layouts  2.87 us (3%)
    pallas_call x1, Pallas kernels, moe(): pl.pallas_call(functools.partial(moe_kernel, n, cap), out_shape=jax.Shape...  74 us
    dot_general x1, matrix products, attention(): jnp.dot(xn, w_q, preferred_element_type=jnp.float32).astype(jnp.bfloat16)  7.07 us
    dot_general x1, matrix products, attention(): jnp.einsum('bhl,blc->bhc', p, cache, preferred_element_type=jnp.float32)  5.85 us
    dot_general x1, matrix products, attention(): jnp.einsum('bhc,blc->bhl', qf, cache, preferred_element_type=jnp.float32)  5.25 us
    dot_general x1, matrix products, attention(): a = jnp.dot(o, w_o, preferred_element_type=jnp.float32)  5.04 us
    dot_general x1, matrix products, attention(): kv = jnp.dot(xn, w_dkv, preferred_element_type=jnp.float32)  2.54 us

profile of v1, /device:TPU:0, one launch (start us, length us, event | category | flops | bytes accessed | tf_op | source)
XLA Modules:
  0.0 111.3 jit_solution(551903903514676100)
XLA Ops:
  0.6 0.7 convert_element_type.69
  1.3 1.0 fusion.16
  2.4 0.7 add_bitcast_fusion
  3.1 0.7 pad.8
  3.8 0.7 iota_compare_fusion
  4.5 0.1 tile.21
  4.6 0.1 tile.9
  4.7 0.6 pad_maximum_fusion.2.meta_ref
  5.3 2.5 %fusion.24 = f32[32,576]{1,0:T(8,128)S(1)} fusion(bf16[2048,576]{0,1:T(8,128)(2,1)} %param.22, bf16[32,2048]{1,0:T(8,128)(2,1)} %param.16, f32[32]{0:T(128)S(1)} %add_rsqrt_fusion.2), kind=kOutput, calls=%fused_computation.41 | convolution fusion | flops 75694080 | bytes 2564224 | tf_op jit(solution)/shard_map/dot_general | solution.py:44
  7.8 0.1 multiply_reduce_fusion
  8.0 0.1 subtract_convert_fusion.1
  8.1 0.1 fusion.30
  8.2 0.1 fusion.38
  8.3 0.7 pad_maximum_fusion.1
  9.0 0.0 copy-start.1
  9.0 7.1 %convolution_convert_fusion = bf16[32,3072]{1,0:T(8,128)(2,1)S(1)} fusion(bf16[2048,3072]{1,0:T(8,128)(2,1)} %param.21, bf16[32,2048]{1,0:T(8,128)(2,1)} %param.16, f32[32]{0:T(128)S(1)} %add_rsqrt_fusion.2), kind=kOutput, calls=%fused_computation.2 | convolution fusion | flops 402948096 | bytes 12910720 | tf_op jit(solution)/shard_map/dot_general | solution.py:43
  16.0 0.3 reshape.149
  16.5 0.1 subtract_convert_fusion
  16.6 0.0 copy-done.1
  16.6 0.4 fusion.3
  17.0 0.1 pad_maximum_fusion
  17.1 0.4 fusion.7
  17.5 5.2 %fusion.31 = (f32[32,16]{1,0:T(8,128)S(1)}, f32[32,16,256]{2,1,0:T(8,128)S(1)}) fusion(bf16[32,256,576]{1,2,0:T(8,128)(2,1)} %param.17, bf16[32,16,576]{2,0,1:T(8,128)(2,1)S(1)} %pad_maximum_fusion, pred[32,256]{1,0:T(8,128)(4,1)S(1)} %iota_compare_fusion), kind=kOutput, calls=%fused_computation.67 | convolution fusion | flops 151387648 | bytes 10561536 | tf_op jit(solution)/shard_map/bhc,blc->bhl/dot_general | solution.py:50
  22.8 0.0 copy-start.2
  22.8 0.0 copy-start
  22.8 0.2 fusion.13
  23.1 0.1 copy.25
  23.1 5.9 %fusion = f32[32,16,512]{2,1,0:T(8,128)S(1)} fusion(bf16[32,256,576]{1,2,0:T(8,128)(2,1)} %param.17, f32[32,16,256]{2,1,0:T(8,128)S(1)} %get-tuple-element.15, f32[32,16]{1,0:T(8,128)S(1)} %get-tuple-element.9, f32[32,16]{1,0:T(8,128)S(1)} %multiply_maximum_fusion), kind=kOutput, calls=%fused_computation | convolution fusion | flops 134610944 | bytes 9965568 | tf_op jit(solution)/shard_map/bhl,blc->bhc/dot_general | solution.py:60
  29.0 0.0 copy-done.2
  29.0 0.9 fusion.5
  29.9 0.0 copy-done
  29.9 5.0 %fusion.14 = (f32[32]{0:T(128)S(1)}, bf16[32,2048]{1,0:T(8,128)(2,1)S(1)}) fusion(bf16[2048,2048]{1,0:T(8,128)(2,1)} %param.25, bf16[16,4,8,128]{3,2,1,0:T(8,128)(2,1)S(1)} %fusion.5, bf16[32,2048]{1,0:T(8,128)(2,1)S(1)} %copy-done), kind=kOutput, calls=%fused_computation.26 | convolution fusion | flops 268828640 | bytes 8781952 | tf_op jit(solution)/shard_map/dot_general | solution.py:63
  34.9 0.0 copy-start.3
  35.0 0.7 fusion.15.u_ref
  35.7 0.0 copy-done.3
  35.7 74.0 %moe.1 = bf16[32,2048]{1,0:T(8,128)(2,1)} custom-call(bf16[32,2048]{1,0:T(8,128)(2,1)} %fusion.15.u_ref, bf16[32,2048]{1,0:T(8,128)(2,1)} %copy-done.3, f32[16,256]{1,0:T(8,128)} %pad_maximum_fusion.2.meta_ref, bf16[8,2048,1408]{2,1,0:T(8,128)(2,1)} %eg.1, bf16[8,2048,1408]{2,1,0:T(8,128)(2,1)} %eu.1, bf16[8,1408,2048]{2,1,0:T(8,128)(2,1)} %ed.1, ...), custom_call_target="tpu_custom_call" | custom-call | flops 7751073792 | bytes 173015040 | tf_op jit(solution)/shard_map/moe/pallas_call | solution.py:353
  109.8 1.6 %copy.56 = bf16[32,2048]{1,0:T(8,128)(2,1)} copy(bf16[32,2048]{1,0:T(8,128)(2,1)} %moe.1) | data formatting | bytes 262144
  (14 shorter events, 0.2 us)
Async XLA Ops:
  9.0 7.6 %copy-start.1 = (bf16[16,128,512]{2,1,0:T(8,128)(2,1)S(1)}, bf16[16,128,512]{2,1,0:T(8,128)(2,1)}, u32[]{:S(2)}) copy-start(bf16[16,128,512]{2,1,0:T(8,128)(2,1)} %param.23) | copy-start | bytes 6291460
  22.8 6.2 %copy-start.2 = (bf16[16,512,128]{2,1,0:T(8,128)(2,1)S(1)}, bf16[16,512,128]{2,1,0:T(8,128)(2,1)}, u32[]{:S(2)}) copy-start(bf16[16,512,128]{2,1,0:T(8,128)(2,1)} %param.24) | copy-start | bytes 6291460
  22.8 7.1 %copy-start = (bf16[32,2048]{1,0:T(8,128)(2,1)S(1)}, bf16[32,2048]{1,0:T(8,128)(2,1)}, u32[]{:S(2)}) copy-start(bf16[32,2048]{1,0:T(8,128)(2,1)} %param.16) | copy-start | bytes 393220
  34.9 0.8 copy-start.3

commit v2 on v1

--- a/solution.py
+++ b/solution.py
@@ -1,4 +1,5 @@
 import functools
+import math
 
 import jax
 import jax.numpy as jnp
@@ -10,63 +11,188 @@
 EPS = 1e-6
 ROPE_BASE = 1.0e4
 CAP_FACTOR = 2
-N_A = 5
-N_B = 3
+N_A = 6
+N_B = 2
 CW = 256
 F32 = jnp.float32
 BF16 = jnp.bfloat16
 
 
-def rms(v):
-    v = v.astype(jnp.float32)
-    return v * lax.rsqrt(jnp.mean(v * v, axis=-1, keepdims=True) + EPS)
-
-
-def rope(v, pos):
-    half = v.shape[-1] // 2
-    inv = ROPE_BASE ** (-2.0 * jnp.arange(half, dtype=jnp.float32) / v.shape[-1])
-    ang = pos.astype(jnp.float32)[..., None] * inv
+def attn_kernel(x_ref, lrow_ref, lens_ref, ids_ref, rw_ref, wq, wdkv, wuk, wuv, wo, cache,
+                h1_ref, u_ref, kvn_ref, meta_ref,
+                wq_b, wdkv_b, wuk_b, wuv_b, wo_b, cache_b, q_s, ql_s, qr_s, kv_s, s_s, p_s, ol_s, o_s, sems):
+    bsz, hid = x_ref.shape
+    heads, nope, kvl = wuk.shape
+    kvd = wdkv.shape[0]
+    rot = kvd - kvl
+    l_max = cache.shape[2]
+    qkd = nope + rot
+    n_q = 3
+    qc = wq.shape[1] // n_q
+    n_c = 4
+    bc = bsz // n_c
+    n_o = 2
+    oc = hid // n_o
+    copies = []
+
+    def start(src, dst):
+        c = pltpu.make_async_copy(src, dst, sems.at[len(copies)])
+        c.start()
+        copies.append(c)
+        return c
+
+    c_q = [start(wq.at[:, i * qc:(i + 1) * qc], wq_b.at[:, i * qc:(i + 1) * qc]) for i in range(n_q)]
+    c_kv = start(wdkv, wdkv_b)
+    c_uk = start(wuk, wuk_b)
+    c_c = [start(cache.at[i * bc:(i + 1) * bc], cache_b.at[i * bc:(i + 1) * bc]) for i in range(n_c)]
+    c_uv = start(wuv, wuv_b)
+    c_o = [start(wo.at[:, i * oc:(i + 1) * oc], wo_b.at[:, i * oc:(i + 1) * oc]) for i in range(n_o)]
+
+    me = lax.axis_index('ep')
+    n_tok = meta_ref.shape[1]
+    top = ids_ref.shape[0]
+    lane = lax.broadcasted_iota(jnp.int32, (top, n_tok), 1) // bsz
+    meta_ref[...] = jnp.zeros_like(meta_ref)
+    for r, v in enumerate((ids_ref[...].astype(F32) + 1.0, rw_ref[...])):
+        v = jnp.concatenate([v] * (n_tok // bsz), axis=1)
+        meta_ref[r * 8:r * 8 + top] = jnp.where(lane == me, v, 0.0)
+
+    eye = lax.broadcasted_iota(jnp.int32, (bsz, bsz), 0) == lax.broadcasted_iota(jnp.int32, (bsz, bsz), 1)
+    pos = jnp.sum(jnp.where(eye, lrow_ref[...].astype(F32), 0.0), axis=1, keepdims=True)
+    half = rot // 2
+    li = lax.broadcasted_iota(jnp.int32, (bsz, rot), 1)
+    fi = jnp.where(li < half, li, li - half).astype(F32)
+    ang = pos * jnp.exp(fi * (-2.0 / rot * math.log(ROPE_BASE)))
     cs = jnp.cos(ang)
     sn = jnp.sin(ang)
-    v1 = v[..., :half]
-    v2 = v[..., half:]
-    return jnp.concatenate([v1 * cs - v2 * sn, v2 * cs + v1 * sn], axis=-1)
-
-
-def attention(x, cache, lens, w_q, w_dkv, w_uk, w_uv, w_o):
-    bsz = x.shape[0]
+    sn = jnp.where(li < half, -sn, sn)
+
+    def rope(v):
+        return v * cs + jnp.concatenate([v[:, half:], v[:, :half]], axis=1) * sn
+
+    def norm(v):
+        return v * lax.rsqrt(jnp.mean(v * v, axis=-1, keepdims=True) + EPS)
+
+    xn = norm(x_ref[...].astype(F32)).astype(BF16)
+    for i in range(n_q):
+        c_q[i].wait()
+        q_s[:, i * qc:(i + 1) * qc] = jnp.dot(
+            xn, wq_b[:, i * qc:(i + 1) * qc], preferred_element_type=F32).astype(BF16)
+    c_kv.wait()
+    kv = lax.dot_general(xn, wdkv_b[...], (((1,), (1,)), ((), ())), preferred_element_type=F32)
+    kvn_ref[:, :kvl] = norm(kv[:, :kvl]).astype(BF16)
+    kvn_ref[:, kvl:] = rope(kv[:, kvl:]).astype(BF16)
+    kv_s[:, :kvd] = kvn_ref[...].astype(F32)
+    c_uk.wait()
+    for h in range(heads):
+        c0 = h * qkd
+        rs = slice(h * bsz, (h + 1) * bsz)
+        ql = jnp.dot(q_s[:, c0:c0 + nope], wuk_b[h], preferred_element_type=F32).astype(BF16).astype(F32)
+        for g in range(kvl // 128):
+            ql_s[g, rs] = ql[:, g * 128:(g + 1) * 128]
+        qr_s[rs, :rot] = rope(q_s[:, c0 + nope:c0 + qkd].astype(F32)).astype(BF16).astype(F32)
+
+    col = lax.broadcasted_iota(jnp.int32, (heads, l_max), 1)
+    scale = qkd ** -0.5
+    unroll = 8
+    for i in range(n_c):
+        c_c[i].wait()
+
+        @pl.loop(0, bc // unroll)
+        def _(t):
+            for k in range(unroll):
+                b = i * bc + t * unroll + k
+                ql = jnp.concatenate(
+                    [ql_s[g, pl.ds(b, heads, stride=bsz), :] for g in range(kvl // 128)], axis=1)
+                qr = qr_s[pl.ds(b, heads, stride=bsz), :][:, :rot]
+                kl = kv_s[pl.ds(b, 1), :]
+                s = jnp.dot(ql.astype(BF16), cache_b[b, :kvl], preferred_element_type=F32)
+                s += jnp.dot(qr.astype(BF16), cache_b[b, kvl:], preferred_element_type=F32)
+                s_new = jnp.sum(ql * kl[:, :kvl], axis=1, keepdims=True)
+                s_new += jnp.sum(qr * kl[:, kvl:kvd], axis=1, keepdims=True)
+                n_live = lens_ref[b]
+                s = jnp.where(col < n_live, s, jnp.where(col == n_live, s_new, -jnp.inf)) * scale
+                s_s[pl.ds(pl.multiple_of(b * heads, heads), heads)] = s
+
+    blk = 128
+
+    @pl.loop(0, bsz * heads // blk)
+    def _(t):
+        rs = pl.ds(pl.multiple_of(t * blk, blk), blk)
+        s = s_s[rs]
+        e = jnp.exp(s - jnp.max(s, axis=1, keepdims=True))
+        p_s[rs] = (e / jnp.sum(e, axis=1, keepdims=True)).astype(BF16)
+
+    @pl.loop(0, bsz // unroll)
+    def _(t):
+        for k in range(unroll):
+            b = t * unroll + k
+            rs = pl.ds(pl.multiple_of(b * heads, heads), heads)
+            n_live = lens_ref[b]
+            p = p_s[rs].astype(F32)
+            p_old = jnp.where(col < n_live, p, 0.0).astype(BF16)
+            p_new = jnp.sum(jnp.where(col == n_live, p, 0.0), axis=1, keepdims=True)
+            o = lax.dot_general(p_old, cache_b[b, :kvl], (((1,), (1,)), ((), ())), preferred_element_type=F32)
+            o += p_new * kv_s[pl.ds(b, 1), :][:, :kvl]
+            o = o.astype(BF16).astype(F32)
+            for g in range(kvl // 128):
+                ol_s[g, rs] = o[:, g * 128:(g + 1) * 128]
+
+    c_uv.wait()
+    vh = wuv.shape[2]
+    for h in range(heads):
+        oh = jnp.concatenate(
+            [ol_s[g, pl.ds(h, bsz, stride=heads), :] for g in range(kvl // 128)], axis=1).astype(BF16)
+        o_s[:, h * vh:(h + 1) * vh] = jnp.dot(oh, wuv_b[h], preferred_element_type=F32).astype(BF16)
+    sq = jnp.zeros((bsz, 1), F32)
+    for i in range(n_o):
+        c_o[i].wait()
+        cols = slice(i * oc, (i + 1) * oc)
+        a = jnp.dot(o_s[...], wo_b[:, cols], preferred_element_type=F32)
+        h1 = (x_ref[:, cols].astype(F32) + a).astype(BF16)
+        h1_ref[:, cols] = h1
+        h1 = h1.astype(F32)
+        sq += jnp.sum(h1 * h1, axis=1, keepdims=True)
+    u_ref[...] = (h1_ref[...].astype(F32) * lax.rsqrt(sq / hid + EPS)).astype(BF16)
+
+
+def attention(n, x, cache, lens, ids, rw, w_q, w_dkv, w_uk, w_uv, w_o):
+    bsz, hid = x.shape
     heads, nope, kvl = w_uk.shape
-    kvd = cache.shape[2]
-    vh = w_uv.shape[2]
-    qkd = nope + kvd - kvl
-    xn = rms(x).astype(jnp.bfloat16)
-    q = jnp.dot(xn, w_q, preferred_element_type=jnp.float32).astype(jnp.bfloat16).reshape(bsz, heads, qkd)
-    kv = jnp.dot(xn, w_dkv, preferred_element_type=jnp.float32)
-    kv_new = jnp.concatenate([rms(kv[:, :kvl]), rope(kv[:, kvl:], lens)], axis=-1).astype(jnp.bfloat16)
-    q_lat = jnp.einsum('bhd,hdc->bhc', q[:, :, :nope], w_uk, preferred_element_type=jnp.float32).astype(jnp.bfloat16)
-    q_rot = rope(q[:, :, nope:].astype(jnp.float32), lens[:, None]).astype(jnp.bfloat16)
-    qf = jnp.concatenate([q_lat, q_rot], axis=-1)
-    scale = qkd ** -0.5
-    s = jnp.einsum('bhc,blc->bhl', qf, cache, preferred_element_type=jnp.float32) * scale
-    live = jnp.arange(cache.shape[1])[None, None, :] < lens[:, None, None]
-    s = jnp.where(live, s, -jnp.inf)
-    s_new = jnp.einsum('bhc,bc->bh', qf, kv_new, preferred_element_type=jnp.float32) * scale
-    mx = jnp.maximum(jnp.max(s, axis=2), s_new)
-    e = jnp.exp(s - mx[:, :, None])
-    e_new = jnp.exp(s_new - mx)
-    den = jnp.sum(e, axis=2) + e_new
-    p = (e / den[:, :, None]).astype(jnp.bfloat16)
-    p_new = (e_new / den).astype(jnp.bfloat16)
-    o_all = jnp.einsum('bhl,blc->bhc', p, cache, preferred_element_type=jnp.float32)
-    o_lat = (o_all[:, :, :kvl] + p_new.astype(jnp.float32)[:, :, None] * kv_new[:, None, :kvl].astype(jnp.float32)).astype(jnp.bfloat16)
-    o = jnp.einsum('bhc,hcv->bhv', o_lat, w_uv, preferred_element_type=jnp.float32).astype(jnp.bfloat16).reshape(bsz, heads * vh)
-    a = jnp.dot(o, w_o, preferred_element_type=jnp.float32)
-    return (x.astype(jnp.float32) + a).astype(jnp.bfloat16), kv_new
+    l_max, kvd = cache.shape[1:]
+    vm = pl.BlockSpec(memory_space=pltpu.VMEM)
+    anys = pl.BlockSpec(memory_space=pl.ANY)
+    cache_t = jnp.swapaxes(cache, 1, 2)
+    rows = bsz * heads
+    weights = (w_q, w_dkv.T, w_uk, w_uv, w_o, cache_t)
+    row = jax.ShapeDtypeStruct((bsz, hid), BF16)
+    return pl.pallas_call(
+        attn_kernel,
+        out_shape=(row, row, jax.ShapeDtypeStruct((bsz, kvd), BF16), jax.ShapeDtypeStruct((16, n * bsz), F32)),
+        in_specs=[vm, vm, pl.BlockSpec(memory_space=pltpu.SMEM), vm, vm] + [anys] * 6,
+        out_specs=(vm,) * 4,
+        scratch_shapes=[pltpu.VMEM(w.shape, BF16) for w in weights] + [
+            pltpu.VMEM((bsz, w_q.shape[1]), BF16),
+            pltpu.VMEM((kvl // 128, rows, 128), F32),
+            pltpu.VMEM((rows, 128), F32),
+            pltpu.VMEM((bsz, kvl + 128), F32),
+            pltpu.VMEM((rows, l_max), F32),
+            pltpu.VMEM((rows, l_max), BF16),
+            pltpu.VMEM((kvl // 128, rows, 128), F32),
+            pltpu.VMEM((bsz, w_o.shape[0]), BF16),
+            pltpu.SemaphoreType.DMA((12,)),
+        ],
+        compiler_params=pltpu.CompilerParams(vmem_limit_bytes=60 << 20),
+        cost_estimate=pl.CostEstimate(
+            flops=2 * bsz * (hid * (w_q.shape[1] + kvd + w_o.shape[0]) + heads * kvl * (2 * nope + 2 * l_max)),
+            bytes_accessed=2 * sum(w.size for w in weights), transcendentals=rows * l_max),
+        name="attn",
+    )(x, lens.reshape(1, bsz), lens, ids.T, rw.T, *weights)
 
 
 def moe_kernel(n, cap, u_ref, h1_ref, meta_ref, eg, eu, ed, sg, su, sd, y_ref,
                wa, wb, meta_all, u_all, xr, act, disp, comb_t, comb, rows,
-               pown, psend, precv, zsum, zrecv, sact,
+               pown, psend, precv, zsum, zside, zrecv, sact,
                sem_a, sem_b, ms, mr, us, ur, fs, fr, ps, pr, zs, zr):
     me = lax.axis_index('ep')
     nz = n // 2
@@ -83,11 +209,15 @@
     def dev(d):
         return {'ep': d}
 
-    def at_z(dz):
-        return lax.rem(zi + dz, nz) * 2 + co
-
-    def from_z(dz):
-        return lax.rem(zi + nz - dz, nz)
+    low = zi < 2
+    inner = jnp.logical_or(zi == 1, zi == 2)
+    beside = jnp.where(low, 1 - zi, 5 - zi)
+    across = jnp.where(low, 2, 1)
+    far = jnp.where(low, 3, 0)
+    others = (far, across, beside)
+
+    def on(z):
+        return dev(z * 2 + co)
 
     def a_copy(src, slot):
         return pltpu.make_async_copy(src, wa.at[slot], sem_a.at[slot])
@@ -139,14 +269,16 @@
 
     def u_copy(k, target):
         return pltpu.make_async_remote_copy(
-            u_ref, u_all.at[my_rows], us.at[k], ur.at[k],
-            device_id=dev(target), device_id_type=pl.DeviceIdType.MESH)
-
-    def fwd_copy(dz):
-        blk = from_z(dz) * 2 + co
-        r = u_all.at[pl.ds(pl.multiple_of(blk * b_dev, b_dev), b_dev)]
+            u_ref, u_all.at[my_rows], us.at[k], ur.at[zi if k < nz - 1 else nz],
+            device_id=target, device_id_type=pl.DeviceIdType.MESH)
+
+    def u_rows(z, c):
+        return u_all.at[pl.ds(pl.multiple_of((z * 2 + c) * b_dev, b_dev), b_dev)]
+
+    def fwd_copy(z):
+        r = u_rows(z, co)
         return pltpu.make_async_remote_copy(
-            r, r, fs.at[dz - 1], fr.at[dz - 1],
+            r, r, fs.at[z], fr.at[z],
             device_id=dev(mate), device_id_type=pl.DeviceIdType.MESH)
 
     def recv_wait(dst, sem):
@@ -156,9 +288,9 @@
 
     for d in range(1, n):
         meta_copy(d).start()
-    for dz in range(1, nz):
-        u_copy(dz - 1, at_z(dz)).start()
-    u_copy(nz - 1, mate).start()
+    for k, z in enumerate(others):
+        u_copy(k, on(z)).start()
+    u_copy(nz - 1, dev(mate)).start()
     u_all[my_rows] = u_ref[...]
 
     tot = meta_ref[...]
@@ -192,21 +324,19 @@
             comb_t[p * slots + e * cap:p * slots + (e + 1) * cap] = jnp.where(m, w[e:e + 1], 0.0).astype(BF16)
     side = r0 // half
     blk = lax.rem(r0, half) // b_dev
-    chip = lax.rem(blk + zi, nz)
+    chip = jnp.where(blk == 0, zi, jnp.where(blk == 1, beside, jnp.where(blk == 2, across, far)))
     core = jnp.where(side == 0, co, 1 - co)
     tok = (chip * 2 + core) * b_dev + lax.rem(r0, b_dev)
     perm = jnp.where(r1 == tok, 1.0, 0.0).astype(BF16)
     comb[...] = lax.dot_general(perm, comb_t[...], (((1,), (1,)), ((), ())),
                                 preferred_element_type=F32).astype(BF16)
 
-    for dz in range(1, nz):
-        blk_z = from_z(dz) * 2 + co
-        recv_wait(u_all.at[pl.ds(pl.multiple_of(blk_z * b_dev, b_dev), b_dev)], ur.at[dz - 1])
-        fwd_copy(dz).start()
-    recv_wait(u_all.at[pl.ds(pl.multiple_of(mate * b_dev, b_dev), b_dev)], ur.at[nz - 1])
-    for dz in range(1, nz):
-        blk_z = from_z(dz) * 2 + 1 - co
-        recv_wait(u_all.at[pl.ds(pl.multiple_of(blk_z * b_dev, b_dev), b_dev)], fr.at[dz - 1])
+    recv_wait(u_rows(zi, 1 - co), ur.at[nz])
+    for z in (beside, across, far):
+        recv_wait(u_rows(z, co), ur.at[z])
+        fwd_copy(z).start()
+    for z in (beside, across, far):
+        recv_wait(u_rows(z, 1 - co), fr.at[z])
 
     @pl.loop(0, hid // 512)
     def _(i):
@@ -258,17 +388,40 @@
             psend.at[j], precv.at[j], ps.at[j], pr.at[j],
             device_id=dev(mate), device_id_type=pl.DeviceIdType.MESH)
 
-    def z_copy(j, dz):
+    def to_beside(j, size):
         return pltpu.make_async_remote_copy(
-            zsum.at[j, pl.ds(dz * b_dev, b_dev)], zrecv.at[j, dz - 1],
-            zs.at[j, dz - 1], zr.at[j, dz - 1],
-            device_id=dev(at_z(dz)), device_id_type=pl.DeviceIdType.MESH)
-
-    def pass_on(j):
+            zsum.at[j, pl.ds(b_dev, size * b_dev)], zside.at[j, pl.ds(0, size * b_dev)],
+            zs.at[j, 0], zr.at[j, 0], device_id=on(beside), device_id_type=pl.DeviceIdType.MESH)
+
+    def to_other(j, k, z):
+        return pltpu.make_async_remote_copy(
+            zsum.at[j, pl.ds((2 + k) * b_dev, b_dev)], zrecv.at[j],
+            zs.at[j, 1 + k], zr.at[j, 1], device_id=on(z), device_id_type=pl.DeviceIdType.MESH)
+
+    def chip_sum(j):
         recv_wait(precv.at[j], pr.at[j])
         zsum[j] = pown[j] + precv[j]
-        for dz in range(1, nz):
-            z_copy(j, dz).start()
+
+        @pl.when(inner)
+        def _():
+            to_beside(j, 1).start()
+
+        @pl.when(jnp.logical_not(inner))
+        def _():
+            to_beside(j, nz - 1).start()
+
+    def wait_beside(j):
+        @pl.when(jnp.logical_not(inner))
+        def _():
+            recv_wait(zside.at[j, pl.ds(0, b_dev)], zr.at[j, 0])
+
+    def relay(j):
+        @pl.when(inner)
+        def _():
+            recv_wait(zside.at[j], zr.at[j, 0])
+            zsum[j, 2 * b_dev:] = zsum[j, 2 * b_dev:] + zside[j, b_dev:]
+            to_other(j, 1, far).start()
+            to_other(j, 0, across).start()
 
     @pl.loop(0, n_ch)
     def _(j):
@@ -299,7 +452,11 @@
 
         @pl.when(j > 0)
         def _():
-            pass_on(lax.max(j - 1, 0))
+            chip_sum(lax.max(j - 1, 0))
+
+        @pl.when(j > 1)
+        def _():
+            relay(lax.max(j - 2, 0))
 
     for h in range(2):
         sa = (n_gu + 2 * h) % N_A
@@ -312,7 +469,10 @@
 
         gate_up(u_ref[...], sa, sb, store)
         if h == 0:
-            pass_on(n_ch - 1)
+            chip_sum(n_ch - 1)
+            relay(n_ch - 2)
+        else:
+            relay(n_ch - 1)
     for h in range(2):
         wait_b((n_ch + h) % N_B)
 
@@ -321,21 +481,31 @@
         s = jnp.dot(sact[:, :inter], wb[n_ch % N_B, :, cols], preferred_element_type=F32)
         s += jnp.dot(sact[:, inter:], wb[(n_ch + 1) % N_B, :, cols], preferred_element_type=F32)
         routed = zsum[j, :b_dev]
-        for dz in range(1, nz):
-            recv_wait(zrecv.at[j, dz - 1], zr.at[j, dz - 1])
-            routed = routed + zrecv[j, dz - 1]
+        wait_beside(j)
+        recv_wait(zrecv.at[j], zr.at[j, 1])
+        routed = routed + zside[j, :b_dev] + zrecv[j]
         y_ref[:, cols] = (h1_ref[:, cols].astype(F32) + s + routed).astype(BF16)
 
     for d in range(1, n):
         meta_copy(d).wait_send()
-    for dz in range(1, nz):
-        u_copy(dz - 1, at_z(dz)).wait_send()
-        fwd_copy(dz).wait_send()
-    u_copy(nz - 1, mate).wait_send()
-    for j in range(n_ch):
+    for k, z in enumerate(others):
+        u_copy(k, on(z)).wait_send()
+        fwd_copy(z).wait_send()
+    u_copy(nz - 1, dev(mate)).wait_send()
+
+    @pl.loop(0, n_ch)
+    def _(j):
         p_copy(j).wait_send()
-        for dz in range(1, nz):
-            z_copy(j, dz).wait_send()
+
+        @pl.when(inner)
+        def _():
+            to_beside(j, 1).wait_send()
+            to_other(j, 0, across).wait_send()
+            to_other(j, 1, far).wait_send()
+
+        @pl.when(jnp.logical_not(inner))
+        def _():
+            to_beside(j, nz - 1).wait_send()
 
 
 def moe(n, u, h1, meta, eg, eu, ed, sg, su, sd, cap):
@@ -370,14 +540,15 @@
             pltpu.VMEM((n_ch, half, CW), F32),
             pltpu.VMEM((n_ch, half, CW), F32),
             pltpu.VMEM((n_ch, half, CW), F32),
-            pltpu.VMEM((n_ch, nz - 1, b_dev, CW), F32),
+            pltpu.VMEM((n_ch, (nz - 1) * b_dev, CW), F32),
+            pltpu.VMEM((n_ch, b_dev, CW), F32),
             pltpu.VMEM((b_dev, 2 * inter), BF16),
             dma((N_A,)), dma((N_B,)),
             dma((n - 1,)), dma((n - 1,)),
+            dma((nz,)), dma((nz + 1,)),
             dma((nz,)), dma((nz,)),
-            dma((nz - 1,)), dma((nz - 1,)),
             dma((n_ch,)), dma((n_ch,)),
-            dma((n_ch, nz - 1)), dma((n_ch, nz - 1)),
+            dma((n_ch, 3)), dma((n_ch, 2)),
         ],
         compiler_params=pltpu.CompilerParams(
             collective_id=0, has_side_effects=True, vmem_limit_bytes=63 << 20),
@@ -398,16 +569,7 @@
         e_loc = e_gate.shape[0]
         n_exp = e_loc * n
         cape = (CAP_FACTOR * b_dev * top + n_exp - 1) // n_exp
-        me = lax.axis_index('ep')
-        here = (jnp.arange(n * b_dev) // b_dev == me)[None]
-        pad = ((0, 8 - top), (0, 0))
-
-        def spread(v):
-            return jnp.where(here, jnp.tile(jnp.pad(v.T, pad), (1, n)), 0.0)
-
-        meta = jnp.concatenate([spread(ids.astype(F32) + 1.0), spread(rw.astype(F32))], axis=0)
-        h1, kv_new = attention(x, cache, lens, w_q, w_dkv, w_uk, w_uv, w_o)
-        u = rms(h1).astype(jnp.bfloat16)
+        h1, u, kv_new, meta = attention(n, x, cache, lens, ids, rw, w_q, w_dkv, w_uk, w_uv, w_o)
         y = moe(n, u, h1, meta, e_gate, e_up, e_down, s_gate, s_up, s_down, n * cape)
         return y, kv_new
 

time: 112 us -> 92.2 us (0.82)
  matrix products: 27.4 us -> 0 us
  Pallas kernels: 74 us -> 89.8 us
  other arithmetic: 6.22 us -> 0 us
  local copies, waits for them, and re-layouts: 2.87 us -> 1.57 us
    dot_general x8 -> x0, matrix products: 27.4 us -> none  [the longest x1 7.07 us: attention(): jnp.dot(xn, w_q, preferred_element_type=jnp.float32).astype(jnp.bfloat16)]
    pallas_call x0 -> x1, Pallas kernels: none -> 16.7 us  [attention(): pl.pallas_call(attn_kernel, out_shape=(row, row, jax.ShapeDtypeStruct((bs...]
    convert_element_type x5 -> x0, other arithmetic: 1.53 us -> none  [the longest x1 0.75 us: local(): u = rms(h1).astype(jnp.bfloat16)]
    concatenate x4 -> x0, other arithmetic: 1.5 us -> none  [the longest x2 0.78 us: attention(): jnp.concatenate([rms(kv[:, :kvl]), rope(kv[:, kvl:], lens)], axis=-1)]
    reduce_sum x3 -> x0, other arithmetic: 1.41 us -> none  [the longest x2 1.16 us: rms(): return v * lax.rsqrt(jnp.mean(v * v, axis=-1, keepdims=True) + EPS)]
where the time goes in v2:
time: 92.2 us; the launch traced here: 92 us
  Pallas kernels  89.8 us (97%)
  local copies, waits for them, and re-layouts  1.57 us (2%)
    pallas_call x1, Pallas kernels, moe(): pl.pallas_call(functools.partial(moe_kernel, n, cap), out_shape=jax.Shape...  73.1 us
    pallas_call x1, Pallas kernels, attention(): pl.pallas_call(attn_kernel, out_shape=(row, row, jax.ShapeDtypeStruct((bs...  16.7 us

profile of v2, /device:TPU:0, one launch (start us, length us, event | category | flops | bytes accessed | tf_op | source)
XLA Modules:
  0.0 92.0 jit_solution(15847158015763555315)
XLA Ops:
  0.6 16.7 %attn.1 = (bf16[32,2048]{1,0:T(8,128)(2,1)}, bf16[32,2048]{1,0:T(8,128)(2,1)}, bf16[32,576]{1,0:T(8,128)(2,1)}, f32[16,256]{1,0:T(8,128)}) custom-call(bf16[32,2048]{1,0:T(8,128)(2,1)} %x_ref.1, s32[1,32]{1,0:T(1,128)} %bitcast.9, s32[32]{0:T(128)} %lens_ref.1, s32[6,32]{1,0:T(8,128)} %bitcast.7, f32[6,32]{1,0:T(8,128)} %bitcast.8, bf16[2048,3072]{1,0:T(8,128)(2,1)} %wq.1, ...), custom_call_target="tpu_custom_call" | custom-call | flops 1149239296 | bytes 36962304 | tf_op jit(solution)/shard_map/attn/pallas_call | solution.py:169
  17.3 73.1 %moe.1 = bf16[32,2048]{1,0:T(8,128)(2,1)} custom-call(bf16[32,2048]{1,0:T(8,128)(2,1)} %get-tuple-element.6.u_ref, bf16[32,2048]{1,0:T(8,128)(2,1)} %get-tuple-element.7.h1_ref, f32[16,256]{1,0:T(8,128)} %get-tuple-element.8.meta_ref, bf16[8,2048,1408]{2,1,0:T(8,128)(2,1)} %eg.1, bf16[8,2048,1408]{2,1,0:T(8,128)(2,1)} %eu.1, bf16[8,1408,2048]{2,1,0:T(8,128)(2,1)} %ed.1, ...), custom_call_target="tpu_custom_call" | custom-call | flops 7751073792 | bytes 173015040 | tf_op jit(solution)/shard_map/moe/pallas_call | solution.py:523
  90.5 1.6 %copy.19 = bf16[32,2048]{1,0:T(8,128)(2,1)} copy(bf16[32,2048]{1,0:T(8,128)(2,1)} %moe.1) | data formatting | bytes 262144

commit v3 on v2

--- a/solution.py
+++ b/solution.py
@@ -18,10 +18,10 @@
 BF16 = jnp.bfloat16
 
 
-def attn_kernel(x_ref, lrow_ref, lens_ref, ids_ref, rw_ref, wq, wdkv, wuk, wuv, wo, cache,
+def attn_kernel(x_in, lrow_in, lens_in, ids_in, rw_in, wq, wdkv, wuk, wuv, wo, cache,
                 h1_ref, u_ref, kvn_ref, meta_ref,
-                wq_b, wdkv_b, wuk_b, wuv_b, wo_b, cache_b, q_s, ql_s, qr_s, kv_s, s_s, p_s, ol_s, o_s, sems):
-    bsz, hid = x_ref.shape
+                x_ref, lrow_ref, lens_ref, ids_ref, rw_ref, wq_b, wdkv_b, wuk_b, wuv_b, wo_b, cache_b, q_s, ql_s, qr_s, kv_s, s_s, p_s, ol_s, o_s, sems):
+    bsz, hid = x_in.shape
     heads, nope, kvl = wuk.shape
     kvd = wdkv.shape[0]
     rot = kvd - kvl
@@ -41,12 +41,18 @@
         copies.append(c)
         return c
 
+    c_x = start(x_in, x_ref)
+    c_small = [start(a, b) for a, b in ((lrow_in, lrow_ref), (lens_in, lens_ref), (ids_in, ids_ref), (rw_in, rw_ref))]
     c_q = [start(wq.at[:, i * qc:(i + 1) * qc], wq_b.at[:, i * qc:(i + 1) * qc]) for i in range(n_q)]
     c_kv = start(wdkv, wdkv_b)
     c_uk = start(wuk, wuk_b)
     c_c = [start(cache.at[i * bc:(i + 1) * bc], cache_b.at[i * bc:(i + 1) * bc]) for i in range(n_c)]
     c_uv = start(wuv, wuv_b)
     c_o = [start(wo.at[:, i * oc:(i + 1) * oc], wo_b.at[:, i * oc:(i + 1) * oc]) for i in range(n_o)]
+
+    c_x.wait()
+    for c in c_small:
+        c.wait()
 
     me = lax.axis_index('ep')
     n_tok = meta_ref.shape[1]
@@ -169,9 +175,15 @@
     return pl.pallas_call(
         attn_kernel,
         out_shape=(row, row, jax.ShapeDtypeStruct((bsz, kvd), BF16), jax.ShapeDtypeStruct((16, n * bsz), F32)),
-        in_specs=[vm, vm, pl.BlockSpec(memory_space=pltpu.SMEM), vm, vm] + [anys] * 6,
+        in_specs=[anys] * 11,
         out_specs=(vm,) * 4,
-        scratch_shapes=[pltpu.VMEM(w.shape, BF16) for w in weights] + [
+        scratch_shapes=[
+            pltpu.VMEM(x.shape, BF16),
+            pltpu.VMEM((1, bsz), jnp.int32),
+            pltpu.SMEM((bsz,), jnp.int32),
+            pltpu.VMEM(ids.shape[::-1], jnp.int32),
+            pltpu.VMEM(rw.shape[::-1], F32),
+        ] + [pltpu.VMEM(w.shape, BF16) for w in weights] + [
             pltpu.VMEM((bsz, w_q.shape[1]), BF16),
             pltpu.VMEM((kvl // 128, rows, 128), F32),
             pltpu.VMEM((rows, 128), F32),
@@ -180,7 +192,7 @@
             pltpu.VMEM((rows, l_max), BF16),
             pltpu.VMEM((kvl // 128, rows, 128), F32),
             pltpu.VMEM((bsz, w_o.shape[0]), BF16),
-            pltpu.SemaphoreType.DMA((12,)),
+            pltpu.SemaphoreType.DMA((17,)),
         ],
         compiler_params=pltpu.CompilerParams(vmem_limit_bytes=60 << 20),
         cost_estimate=pl.CostEstimate(
@@ -190,10 +202,10 @@
     )(x, lens.reshape(1, bsz), lens, ids.T, rw.T, *weights)
 
 
-def moe_kernel(n, cap, u_ref, h1_ref, meta_ref, eg, eu, ed, sg, su, sd, y_ref,
-               wa, wb, meta_all, u_all, xr, act, disp, comb_t, comb, rows,
+def moe_kernel(n, cap, u_in, h1_in, meta_in, eg, eu, ed, sg, su, sd, y_ref,
+               u_ref, h1_ref, meta_ref, wa, wb, meta_all, u_all, xr, act, disp, comb_t, comb, rows,
                pown, psend, precv, zsum, zside, zrecv, sact,
-               sem_a, sem_b, ms, mr, us, ur, fs, fr, ps, pr, zs, zr):
+               sem_i, sem_a, sem_b, ms, mr, us, ur, fs, fr, ps, pr, zs, zr):
     me = lax.axis_index('ep')
     nz = n // 2
     zi = me // 2
@@ -250,6 +262,10 @@
             r, h = sh_a[i - n_gu]
             a_copy(r.at[:, pl.ds(h * inter, inter)], slot).start()
 
+    small = [pltpu.make_async_copy(src, dst, sem_i.at[i]) for i, (src, dst) in enumerate(
+        ((u_in, u_ref), (meta_in, meta_ref), (h1_in, h1_ref)))]
+    for c in small:
+        c.start()
     for i in range(N_A):
         start_unit_a(i)
     for j in range(N_B):
@@ -258,6 +274,8 @@
     barrier = pltpu.get_barrier_semaphore()
     for d in range(1, n):
         pl.semaphore_signal(barrier, inc=1, device_id=dev(lax.rem(me + d, n)))
+    for c in small:
+        c.wait()
     pl.semaphore_wait(barrier, n - 1)
 
     def meta_copy(d):
@@ -377,11 +395,6 @@
             def _():
                 a_copy(eu.at[lax.min(i // 2, e_loc - 1)], slot).start()
 
-            for q in range(4):
-                @pl.when(i == n_gu + q)
-                def _():
-                    r, h = sh_a[q]
-                    a_copy(r.at[:, pl.ds(h * inter, inter)], slot).start()
 
     def p_copy(j):
         return pltpu.make_async_remote_copy(
@@ -443,6 +456,11 @@
             def _():
                 pltpu.make_async_copy(sd.at[pl.ds(h * inter, inter)], wb.at[i % N_B], sem_b.at[i % N_B]).start()
 
+        @pl.when(j + N_B == n_ch - 1)
+        def _():
+            for i in range(n_gu, n_gu + len(sh_a)):
+                start_unit_a(i)
+
         part = jnp.dot(comb[:, 0:slots], rows[...], preferred_element_type=F32)
         part += jnp.dot(comb[:, slots:2 * slots], rows[...], preferred_element_type=F32)
         part += jnp.dot(comb[:, 2 * slots:3 * slots], rows[...], preferred_element_type=F32)
@@ -458,6 +476,9 @@
         def _():
             relay(lax.max(j - 2, 0))
 
+    chip_sum(n_ch - 1)
+    relay(n_ch - 2)
+
     for h in range(2):
         sa = (n_gu + 2 * h) % N_A
         sb = (n_gu + 2 * h + 1) % N_A
@@ -469,9 +490,6 @@
 
         gate_up(u_ref[...], sa, sb, store)
         if h == 0:
-            chip_sum(n_ch - 1)
-            relay(n_ch - 2)
-        else:
             relay(n_ch - 1)
     for h in range(2):
         wait_b((n_ch + h) % N_B)
@@ -523,9 +541,12 @@
     return pl.pallas_call(
         functools.partial(moe_kernel, n, cap),
         out_shape=jax.ShapeDtypeStruct((b_dev, hid), BF16),
-        in_specs=[vm, vm, vm] + [anys] * 6,
+        in_specs=[anys] * 9,
         out_specs=vm,
         scratch_shapes=[
+            pltpu.VMEM(u.shape, BF16),
+            pltpu.VMEM(u.shape, BF16),
+            pltpu.VMEM(meta.shape, F32),
             pltpu.VMEM((N_A, hid, inter), BF16),
             pltpu.VMEM((N_B, inter, hid), BF16),
             pltpu.VMEM((n,) + meta.shape, F32),
@@ -543,7 +564,7 @@
             pltpu.VMEM((n_ch, (nz - 1) * b_dev, CW), F32),
             pltpu.VMEM((n_ch, b_dev, CW), F32),
             pltpu.VMEM((b_dev, 2 * inter), BF16),
-            dma((N_A,)), dma((N_B,)),
+            dma((3,)), dma((N_A,)), dma((N_B,)),
             dma((n - 1,)), dma((n - 1,)),
             dma((nz,)), dma((nz + 1,)),
             dma((nz,)), dma((nz,)),

time: 92.2 us -> 101 us (1.095); the launches traced: 92 us -> 99.4 us
  Pallas kernels: 89.8 us -> 97.2 us
    pallas_call x1, Pallas kernels: 73.1 us -> 81.3 us  [moe(): pl.pallas_call(functools.partial(moe_kernel, n, cap), out_shape=jax.Shape...]
where the time goes in v3:
time: 101 us; the launch traced here: 99.4 us
  Pallas kernels  97.2 us (96%)
  local copies, waits for them, and re-layouts  1.57 us (2%)
    pallas_call x1, Pallas kernels, moe(): pl.pallas_call(functools.partial(moe_kernel, n, cap), out_shape=jax.Shape...  81.3 us
    pallas_call x1, Pallas kernels, attention(): pl.pallas_call(attn_kernel, out_shape=(row, row, jax.ShapeDtypeStruct((bs...  15.9 us

profile of v3, /device:TPU:0, one launch (start us, length us, event | category | flops | bytes accessed | tf_op | source)
XLA Modules:
  0.0 99.4 jit_solution(1322716749085096921)
XLA Ops:
  0.6 15.9 %attn.1 = (bf16[32,2048]{1,0:T(8,128)(2,1)}, bf16[32,2048]{1,0:T(8,128)(2,1)}, bf16[32,576]{1,0:T(8,128)(2,1)}, f32[16,256]{1,0:T(8,128)}) custom-call(bf16[32,2048]{1,0:T(8,128)(2,1)} %x_in.1, s32[1,32]{1,0:T(1,128)} %bitcast.9, s32[32]{0:T(128)} %lens_in.1, s32[6,32]{1,0:T(8,128)} %bitcast.7, f32[6,32]{1,0:T(8,128)} %bitcast.8, bf16[2048,3072]{1,0:T(8,128)(2,1)} %wq.1, ...), custom_call_target="tpu_custom_call" | custom-call | flops 1149239296 | bytes 36962304 | tf_op jit(solution)/shard_map/attn/pallas_call | solution.py:175
  16.6 81.3 %moe.1 = bf16[32,2048]{1,0:T(8,128)(2,1)} custom-call(bf16[32,2048]{1,0:T(8,128)(2,1)} %get-tuple-element.6.u_in, bf16[32,2048]{1,0:T(8,128)(2,1)} %get-tuple-element.7.h1_in, f32[16,256]{1,0:T(8,128)} %get-tuple-element.8.meta_in, bf16[8,2048,1408]{2,1,0:T(8,128)(2,1)} %eg.1, bf16[8,2048,1408]{2,1,0:T(8,128)(2,1)} %eu.1, bf16[8,1408,2048]{2,1,0:T(8,128)(2,1)} %ed.1, ...), custom_call_target="tpu_custom_call" | custom-call | flops 7751073792 | bytes 173015040 | tf_op jit(solution)/shard_map/moe/pallas_call | solution.py:541
  97.8 1.6 %copy.19 = bf16[32,2048]{1,0:T(8,128)(2,1)} copy(bf16[32,2048]{1,0:T(8,128)(2,1)} %moe.1) | data formatting | bytes 262144

commit v4 on v3

--- a/solution.py
+++ b/solution.py
@@ -204,7 +204,7 @@
 
 def moe_kernel(n, cap, u_in, h1_in, meta_in, eg, eu, ed, sg, su, sd, y_ref,
                u_ref, h1_ref, meta_ref, wa, wb, meta_all, u_all, xr, act, disp, comb_t, comb, rows,
-               pown, psend, precv, zsum, zside, zrecv, sact,
+               pown, psend, precv, zsum, zside, zrecv, sact, own,
                sem_i, sem_a, sem_b, ms, mr, us, ur, fs, fr, ps, pr, zs, zr):
     me = lax.axis_index('ep')
     nz = n // 2
@@ -395,6 +395,10 @@
             def _():
                 a_copy(eu.at[lax.min(i // 2, e_loc - 1)], slot).start()
 
+            for q in range(2):
+                @pl.when(i == n_gu + q)
+                def _():
+                    start_unit_a(n_gu + q)
 
     def p_copy(j):
         return pltpu.make_async_remote_copy(
@@ -456,10 +460,10 @@
             def _():
                 pltpu.make_async_copy(sd.at[pl.ds(h * inter, inter)], wb.at[i % N_B], sem_b.at[i % N_B]).start()
 
-        @pl.when(j + N_B == n_ch - 1)
-        def _():
-            for i in range(n_gu, n_gu + len(sh_a)):
-                start_unit_a(i)
+        for q in range(2):
+            @pl.when(j == 2 + q)
+            def _():
+                start_unit_a(n_gu + 2 + q)
 
         part = jnp.dot(comb[:, 0:slots], rows[...], preferred_element_type=F32)
         part += jnp.dot(comb[:, slots:2 * slots], rows[...], preferred_element_type=F32)
@@ -472,12 +476,12 @@
         def _():
             chip_sum(lax.max(j - 1, 0))
 
-        @pl.when(j > 1)
-        def _():
-            relay(lax.max(j - 2, 0))
+        for k, at in enumerate((4, 5, 7)):
+            @pl.when(j == at)
+            def _():
+                relay(k)
 
     chip_sum(n_ch - 1)
-    relay(n_ch - 2)
 
     for h in range(2):
         sa = (n_gu + 2 * h) % N_A
@@ -489,8 +493,8 @@
             sact[:, h * inter + c0:h * inter + c1] = val
 
         gate_up(u_ref[...], sa, sb, store)
-        if h == 0:
-            relay(n_ch - 1)
+        relay(3 + 2 * h)
+        relay(4 + 2 * h)
     for h in range(2):
         wait_b((n_ch + h) % N_B)
 
@@ -498,11 +502,14 @@
         cols = slice(j * CW, (j + 1) * CW)
         s = jnp.dot(sact[:, :inter], wb[n_ch % N_B, :, cols], preferred_element_type=F32)
         s += jnp.dot(sact[:, inter:], wb[(n_ch + 1) % N_B, :, cols], preferred_element_type=F32)
-        routed = zsum[j, :b_dev]
+        own[:, cols] = h1_ref[:, cols].astype(F32) + s
+    relay(n_ch - 1)
+    for j in range(n_ch):
+        cols = slice(j * CW, (j + 1) * CW)
         wait_beside(j)
         recv_wait(zrecv.at[j], zr.at[j, 1])
-        routed = routed + zside[j, :b_dev] + zrecv[j]
-        y_ref[:, cols] = (h1_ref[:, cols].astype(F32) + s + routed).astype(BF16)
+        routed = zsum[j, :b_dev] + zside[j, :b_dev] + zrecv[j]
+        y_ref[:, cols] = (own[:, cols] + routed).astype(BF16)
 
     for d in range(1, n):
         meta_copy(d).wait_send()
@@ -564,6 +571,7 @@
             pltpu.VMEM((n_ch, (nz - 1) * b_dev, CW), F32),
             pltpu.VMEM((n_ch, b_dev, CW), F32),
             pltpu.VMEM((b_dev, 2 * inter), BF16),
+            pltpu.VMEM((b_dev, hid), F32),
             dma((3,)), dma((N_A,)), dma((N_B,)),
             dma((n - 1,)), dma((n - 1,)),
             dma((nz,)), dma((nz + 1,)),

time: 101 us -> 104 us (1.030); the launches traced: 99.4 us -> 104 us
  Pallas kernels: 97.2 us -> 101 us
    pallas_call x1, Pallas kernels: 81.3 us -> 85.5 us  [moe(): pl.pallas_call(functools.partial(moe_kernel, n, cap), out_shape=jax.Shape...]
where the time goes in v4:
time: 104 us
  Pallas kernels  101 us (97%)
  local copies, waits for them, and re-layouts  1.57 us (2%)
    pallas_call x1, Pallas kernels, moe(): pl.pallas_call(functools.partial(moe_kernel, n, cap), out_shape=jax.Shape...  85.5 us
    pallas_call x1, Pallas kernels, attention(): pl.pallas_call(attn_kernel, out_shape=(row, row, jax.ShapeDtypeStruct((bs...  15.9 us

profile of v4, /device:TPU:0, one launch (start us, length us, event | category | flops | bytes accessed | tf_op | source)
XLA Modules:
  0.0 103.6 jit_solution(2704603167687565359)
XLA Ops:
  0.6 15.9 %attn.1 = (bf16[32,2048]{1,0:T(8,128)(2,1)}, bf16[32,2048]{1,0:T(8,128)(2,1)}, bf16[32,576]{1,0:T(8,128)(2,1)}, f32[16,256]{1,0:T(8,128)}) custom-call(bf16[32,2048]{1,0:T(8,128)(2,1)} %x_in.1, s32[1,32]{1,0:T(1,128)} %bitcast.9, s32[32]{0:T(128)} %lens_in.1, s32[6,32]{1,0:T(8,128)} %bitcast.7, f32[6,32]{1,0:T(8,128)} %bitcast.8, bf16[2048,3072]{1,0:T(8,128)(2,1)} %wq.1, ...), custom_call_target="tpu_custom_call" | custom-call | flops 1149239296 | bytes 36962304 | tf_op jit(solution)/shard_map/attn/pallas_call | solution.py:175
  16.6 85.5 %moe.1 = bf16[32,2048]{1,0:T(8,128)(2,1)} custom-call(bf16[32,2048]{1,0:T(8,128)(2,1)} %get-tuple-element.6.u_in, bf16[32,2048]{1,0:T(8,128)(2,1)} %get-tuple-element.7.h1_in, f32[16,256]{1,0:T(8,128)} %get-tuple-element.8.meta_in, bf16[8,2048,1408]{2,1,0:T(8,128)(2,1)} %eg.1, bf16[8,2048,1408]{2,1,0:T(8,128)(2,1)} %eu.1, bf16[8,1408,2048]{2,1,0:T(8,128)(2,1)} %ed.1, ...), custom_call_target="tpu_custom_call" | custom-call | flops 7751073792 | bytes 173015040 | tf_op jit(solution)/shard_map/moe/pallas_call | solution.py:548
  102.0 1.6 %copy.19 = bf16[32,2048]{1,0:T(8,128)(2,1)} copy(bf16[32,2048]{1,0:T(8,128)(2,1)} %moe.1) | data formatting | bytes 262144

commit v5 on v4

--- a/solution.py
+++ b/solution.py
@@ -234,10 +234,6 @@
     def a_copy(src, slot):
         return pltpu.make_async_copy(src, wa.at[slot], sem_a.at[slot])
 
-    def start_gu(e, k):
-        a_copy(eg.at[e], lax.rem(2 * e, N_A)).start()
-        a_copy(eu.at[e], lax.rem(2 * e + 1, N_A)).start()
-
     def start_down(j):
         slot = lax.rem(j, N_B)
         for e in range(e_loc):
@@ -266,11 +262,6 @@
         ((u_in, u_ref), (meta_in, meta_ref), (h1_in, h1_ref)))]
     for c in small:
         c.start()
-    for i in range(N_A):
-        start_unit_a(i)
-    for j in range(N_B):
-        start_down(j)
-
     barrier = pltpu.get_barrier_semaphore()
     for d in range(1, n):
         pl.semaphore_signal(barrier, inc=1, device_id=dev(lax.rem(me + d, n)))
@@ -309,6 +300,8 @@
     for k, z in enumerate(others):
         u_copy(k, on(z)).start()
     u_copy(nz - 1, dev(mate)).start()
+    for i in range(N_A):
+        start_unit_a(i)
     u_all[my_rows] = u_ref[...]
 
     tot = meta_ref[...]
@@ -356,6 +349,9 @@
     for z in (beside, across, far):
         recv_wait(u_rows(z, 1 - co), fr.at[z])
 
+    for j in range(N_B):
+        start_down(j)
+
     @pl.loop(0, hid // 512)
     def _(i):
         cols = pl.ds(pl.multiple_of(i * 512, 512), 512)
@@ -449,22 +445,6 @@
                 act[e * cap:(e + 1) * cap], wb[slot, :, e * CW:(e + 1) * CW],
                 preferred_element_type=F32).astype(BF16)
 
-        @pl.when(j + N_B < n_ch)
-        def _():
-            start_down(lax.min(j + N_B, n_ch - 1))
-
-        for h in range(2):
-            i = n_ch + h
-
-            @pl.when(j + N_B == i)
-            def _():
-                pltpu.make_async_copy(sd.at[pl.ds(h * inter, inter)], wb.at[i % N_B], sem_b.at[i % N_B]).start()
-
-        for q in range(2):
-            @pl.when(j == 2 + q)
-            def _():
-                start_unit_a(n_gu + 2 + q)
-
         part = jnp.dot(comb[:, 0:slots], rows[...], preferred_element_type=F32)
         part += jnp.dot(comb[:, slots:2 * slots], rows[...], preferred_element_type=F32)
         part += jnp.dot(comb[:, 2 * slots:3 * slots], rows[...], preferred_element_type=F32)
@@ -472,16 +452,33 @@
         psend[j] = part[half:]
         p_copy(j).start()
 
-        @pl.when(j > 0)
-        def _():
-            chip_sum(lax.max(j - 1, 0))
-
-        for k, at in enumerate((4, 5, 7)):
-            @pl.when(j == at)
+        @pl.when(j > 1)
+        def _():
+            chip_sum(lax.max(j - 2, 0))
+
+        @pl.when(j > 4)
+        def _():
+            relay(lax.max(j - 5, 0))
+
+        @pl.when(j + N_B < n_ch)
+        def _():
+            start_down(lax.min(j + N_B, n_ch - 1))
+
+        for h in range(2):
+            i = n_ch + h
+
+            @pl.when(j + N_B == i)
             def _():
-                relay(k)
-
+                pltpu.make_async_copy(sd.at[pl.ds(h * inter, inter)], wb.at[i % N_B], sem_b.at[i % N_B]).start()
+
+        @pl.when(j + N_B == n_ch - 1)
+        def _():
+            for q in range(2):
+                start_unit_a(n_gu + 2 + q)
+
+    chip_sum(n_ch - 2)
     chip_sum(n_ch - 1)
+    relay(n_ch - 5)
 
     for h in range(2):
         sa = (n_gu + 2 * h) % N_A
@@ -493,8 +490,8 @@
             sact[:, h * inter + c0:h * inter + c1] = val
 
         gate_up(u_ref[...], sa, sb, store)
-        relay(3 + 2 * h)
-        relay(4 + 2 * h)
+        relay(n_ch - 4 + 2 * h)
+        relay(n_ch - 3 + 2 * h)
     for h in range(2):
         wait_b((n_ch + h) % N_B)
 
@@ -503,7 +500,6 @@
         s = jnp.dot(sact[:, :inter], wb[n_ch % N_B, :, cols], preferred_element_type=F32)
         s += jnp.dot(sact[:, inter:], wb[(n_ch + 1) % N_B, :, cols], preferred_element_type=F32)
         own[:, cols] = h1_ref[:, cols].astype(F32) + s
-    relay(n_ch - 1)
     for j in range(n_ch):
         cols = slice(j * CW, (j + 1) * CW)
         wait_beside(j)

time: 104 us -> 91.9 us (0.88)
  Pallas kernels: 101 us -> 89.5 us
    pallas_call x1, Pallas kernels: 85.5 us -> 73.6 us  [moe(): pl.pallas_call(functools.partial(moe_kernel, n, cap), out_shape=jax.Shape...]
where the time goes in v5:
time: 91.9 us; the launch traced here: 91.7 us
  Pallas kernels  89.5 us (97%)
  local copies, waits for them, and re-layouts  1.57 us (2%)
    pallas_call x1, Pallas kernels, moe(): pl.pallas_call(functools.partial(moe_kernel, n, cap), out_shape=jax.Shape...  73.6 us
    pallas_call x1, Pallas kernels, attention(): pl.pallas_call(attn_kernel, out_shape=(row, row, jax.ShapeDtypeStruct((bs...  15.9 us

profile of v5, /device:TPU:0, one launch (start us, length us, event | category | flops | bytes accessed | tf_op | source)
XLA Modules:
  0.0 91.7 jit_solution(7572223492350397973)
XLA Ops:
  0.6 15.9 %attn.1 = (bf16[32,2048]{1,0:T(8,128)(2,1)}, bf16[32,2048]{1,0:T(8,128)(2,1)}, bf16[32,576]{1,0:T(8,128)(2,1)}, f32[16,256]{1,0:T(8,128)}) custom-call(bf16[32,2048]{1,0:T(8,128)(2,1)} %x_in.1, s32[1,32]{1,0:T(1,128)} %bitcast.9, s32[32]{0:T(128)} %lens_in.1, s32[6,32]{1,0:T(8,128)} %bitcast.7, f32[6,32]{1,0:T(8,128)} %bitcast.8, bf16[2048,3072]{1,0:T(8,128)(2,1)} %wq.1, ...), custom_call_target="tpu_custom_call" | custom-call | flops 1149239296 | bytes 36962304 | tf_op jit(solution)/shard_map/attn/pallas_call | solution.py:175
  16.6 73.6 %moe.1 = bf16[32,2048]{1,0:T(8,128)(2,1)} custom-call(bf16[32,2048]{1,0:T(8,128)(2,1)} %get-tuple-element.6.u_in, bf16[32,2048]{1,0:T(8,128)(2,1)} %get-tuple-element.7.h1_in, f32[16,256]{1,0:T(8,128)} %get-tuple-element.8.meta_in, bf16[8,2048,1408]{2,1,0:T(8,128)(2,1)} %eg.1, bf16[8,2048,1408]{2,1,0:T(8,128)(2,1)} %eu.1, bf16[8,1408,2048]{2,1,0:T(8,128)(2,1)} %ed.1, ...), custom_call_target="tpu_custom_call" | custom-call | flops 7751073792 | bytes 173015040 | tf_op jit(solution)/shard_map/moe/pallas_call | solution.py:544
  90.2 1.6 %copy.19 = bf16[32,2048]{1,0:T(8,128)(2,1)} copy(bf16[32,2048]{1,0:T(8,128)(2,1)} %moe.1) | data formatting | bytes 262144

commit v6 on v3

--- a/solution.py
+++ b/solution.py
@@ -11,8 +11,8 @@
 EPS = 1e-6
 ROPE_BASE = 1.0e4
 CAP_FACTOR = 2
-N_A = 6
-N_B = 2
+N_A = 5
+N_B = 3
 CW = 256
 F32 = jnp.float32
 BF16 = jnp.bfloat16
@@ -204,7 +204,7 @@
 
 def moe_kernel(n, cap, u_in, h1_in, meta_in, eg, eu, ed, sg, su, sd, y_ref,
                u_ref, h1_ref, meta_ref, wa, wb, meta_all, u_all, xr, act, disp, comb_t, comb, rows,
-               pown, psend, precv, zsum, zside, zrecv, sact,
+               pown, psend, precv, zsum, zrecv, sact,
                sem_i, sem_a, sem_b, ms, mr, us, ur, fs, fr, ps, pr, zs, zr):
     me = lax.axis_index('ep')
     nz = n // 2
@@ -221,22 +221,14 @@
     def dev(d):
         return {'ep': d}
 
-    low = zi < 2
-    inner = jnp.logical_or(zi == 1, zi == 2)
-    beside = jnp.where(low, 1 - zi, 5 - zi)
-    across = jnp.where(low, 2, 1)
-    far = jnp.where(low, 3, 0)
-    others = (far, across, beside)
-
-    def on(z):
-        return dev(z * 2 + co)
+    def at_z(dz):
+        return lax.rem(zi + dz, nz) * 2 + co
+
+    def from_z(dz):
+        return lax.rem(zi + nz - dz, nz)
 
     def a_copy(src, slot):
         return pltpu.make_async_copy(src, wa.at[slot], sem_a.at[slot])
-
-    def start_gu(e, k):
-        a_copy(eg.at[e], lax.rem(2 * e, N_A)).start()
-        a_copy(eu.at[e], lax.rem(2 * e + 1, N_A)).start()
 
     def start_down(j):
         slot = lax.rem(j, N_B)
@@ -266,11 +258,6 @@
         ((u_in, u_ref), (meta_in, meta_ref), (h1_in, h1_ref)))]
     for c in small:
         c.start()
-    for i in range(N_A):
-        start_unit_a(i)
-    for j in range(N_B):
-        start_down(j)
-
     barrier = pltpu.get_barrier_semaphore()
     for d in range(1, n):
         pl.semaphore_signal(barrier, inc=1, device_id=dev(lax.rem(me + d, n)))
@@ -287,16 +274,14 @@
 
     def u_copy(k, target):
         return pltpu.make_async_remote_copy(
-            u_ref, u_all.at[my_rows], us.at[k], ur.at[zi if k < nz - 1 else nz],
-            device_id=target, device_id_type=pl.DeviceIdType.MESH)
-
-    def u_rows(z, c):
-        return u_all.at[pl.ds(pl.multiple_of((z * 2 + c) * b_dev, b_dev), b_dev)]
-
-    def fwd_copy(z):
-        r = u_rows(z, co)
+            u_ref, u_all.at[my_rows], us.at[k], ur.at[k],
+            device_id=dev(target), device_id_type=pl.DeviceIdType.MESH)
+
+    def fwd_copy(dz):
+        blk = from_z(dz) * 2 + co
+        r = u_all.at[pl.ds(pl.multiple_of(blk * b_dev, b_dev), b_dev)]
         return pltpu.make_async_remote_copy(
-            r, r, fs.at[z], fr.at[z],
+            r, r, fs.at[dz - 1], fr.at[dz - 1],
             device_id=dev(mate), device_id_type=pl.DeviceIdType.MESH)
 
     def recv_wait(dst, sem):
@@ -306,9 +291,13 @@
 
     for d in range(1, n):
         meta_copy(d).start()
-    for k, z in enumerate(others):
-        u_copy(k, on(z)).start()
-    u_copy(nz - 1, dev(mate)).start()
+    for dz in (2, 1, 3):
+        u_copy(dz - 1, at_z(dz)).start()
+    u_copy(nz - 1, mate).start()
+    for i in range(N_A):
+        start_unit_a(i)
+    for j in range(N_B):
+        start_down(j)
     u_all[my_rows] = u_ref[...]
 
     tot = meta_ref[...]
@@ -342,19 +331,21 @@
             comb_t[p * slots + e * cap:p * slots + (e + 1) * cap] = jnp.where(m, w[e:e + 1], 0.0).astype(BF16)
     side = r0 // half
     blk = lax.rem(r0, half) // b_dev
-    chip = jnp.where(blk == 0, zi, jnp.where(blk == 1, beside, jnp.where(blk == 2, across, far)))
+    chip = lax.rem(blk + zi, nz)
     core = jnp.where(side == 0, co, 1 - co)
     tok = (chip * 2 + core) * b_dev + lax.rem(r0, b_dev)
     perm = jnp.where(r1 == tok, 1.0, 0.0).astype(BF16)
     comb[...] = lax.dot_general(perm, comb_t[...], (((1,), (1,)), ((), ())),
                                 preferred_element_type=F32).astype(BF16)
 
-    recv_wait(u_rows(zi, 1 - co), ur.at[nz])
-    for z in (beside, across, far):
-        recv_wait(u_rows(z, co), ur.at[z])
-        fwd_copy(z).start()
-    for z in (beside, across, far):
-        recv_wait(u_rows(z, 1 - co), fr.at[z])
+    for dz in range(1, nz):
+        blk_z = from_z(dz) * 2 + co
+        recv_wait(u_all.at[pl.ds(pl.multiple_of(blk_z * b_dev, b_dev), b_dev)], ur.at[dz - 1])
+        fwd_copy(dz).start()
+    recv_wait(u_all.at[pl.ds(pl.multiple_of(mate * b_dev, b_dev), b_dev)], ur.at[nz - 1])
+    for dz in range(1, nz):
+        blk_z = from_z(dz) * 2 + 1 - co
+        recv_wait(u_all.at[pl.ds(pl.multiple_of(blk_z * b_dev, b_dev), b_dev)], fr.at[dz - 1])
 
     @pl.loop(0, hid // 512)
     def _(i):
@@ -395,46 +386,28 @@
             def _():
                 a_copy(eu.at[lax.min(i // 2, e_loc - 1)], slot).start()
 
+            for q in range(4):
+                @pl.when(i == n_gu + q)
+                def _():
+                    r, h = sh_a[q]
+                    a_copy(r.at[:, pl.ds(h * inter, inter)], slot).start()
 
     def p_copy(j):
         return pltpu.make_async_remote_copy(
             psend.at[j], precv.at[j], ps.at[j], pr.at[j],
             device_id=dev(mate), device_id_type=pl.DeviceIdType.MESH)
 
-    def to_beside(j, size):
+    def z_copy(j, dz):
         return pltpu.make_async_remote_copy(
-            zsum.at[j, pl.ds(b_dev, size * b_dev)], zside.at[j, pl.ds(0, size * b_dev)],
-            zs.at[j, 0], zr.at[j, 0], device_id=on(beside), device_id_type=pl.DeviceIdType.MESH)
-
-    def to_other(j, k, z):
-        return pltpu.make_async_remote_copy(
-            zsum.at[j, pl.ds((2 + k) * b_dev, b_dev)], zrecv.at[j],
-            zs.at[j, 1 + k], zr.at[j, 1], device_id=on(z), device_id_type=pl.DeviceIdType.MESH)
-
-    def chip_sum(j):
+            zsum.at[j, pl.ds(dz * b_dev, b_dev)], zrecv.at[j, dz - 1],
+            zs.at[j, dz - 1], zr.at[j, dz - 1],
+            device_id=dev(at_z(dz)), device_id_type=pl.DeviceIdType.MESH)
+
+    def pass_on(j):
         recv_wait(precv.at[j], pr.at[j])
         zsum[j] = pown[j] + precv[j]
-
-        @pl.when(inner)
-        def _():
-            to_beside(j, 1).start()
-
-        @pl.when(jnp.logical_not(inner))
-        def _():
-            to_beside(j, nz - 1).start()
-
-    def wait_beside(j):
-        @pl.when(jnp.logical_not(inner))
-        def _():
-            recv_wait(zside.at[j, pl.ds(0, b_dev)], zr.at[j, 0])
-
-    def relay(j):
-        @pl.when(inner)
-        def _():
-            recv_wait(zside.at[j], zr.at[j, 0])
-            zsum[j, 2 * b_dev:] = zsum[j, 2 * b_dev:] + zside[j, b_dev:]
-            to_other(j, 1, far).start()
-            to_other(j, 0, across).start()
+        for dz in range(1, nz):
+            z_copy(j, dz).start()
 
     @pl.loop(0, n_ch)
     def _(j):
@@ -456,11 +429,6 @@
             def _():
                 pltpu.make_async_copy(sd.at[pl.ds(h * inter, inter)], wb.at[i % N_B], sem_b.at[i % N_B]).start()
 
-        @pl.when(j + N_B == n_ch - 1)
-        def _():
-            for i in range(n_gu, n_gu + len(sh_a)):
-                start_unit_a(i)
-
         part = jnp.dot(comb[:, 0:slots], rows[...], preferred_element_type=F32)
         part += jnp.dot(comb[:, slots:2 * slots], rows[...], preferred_element_type=F32)
         part += jnp.dot(comb[:, 2 * slots:3 * slots], rows[...], preferred_element_type=F32)
@@ -470,14 +438,7 @@
 
         @pl.when(j > 0)
         def _():
-            chip_sum(lax.max(j - 1, 0))
-
-        @pl.when(j > 1)
-        def _():
-            relay(lax.max(j - 2, 0))
-
-    chip_sum(n_ch - 1)
-    relay(n_ch - 2)
+            pass_on(lax.max(j - 1, 0))
 
     for h in range(2):
         sa = (n_gu + 2 * h) % N_A
@@ -490,7 +451,7 @@
 
         gate_up(u_ref[...], sa, sb, store)
         if h == 0:
-            relay(n_ch - 1)
+            pass_on(n_ch - 1)
     for h in range(2):
         wait_b((n_ch + h) % N_B)
 
@@ -499,31 +460,21 @@
         s = jnp.dot(sact[:, :inter], wb[n_ch % N_B, :, cols], preferred_element_type=F32)
         s += jnp.dot(sact[:, inter:], wb[(n_ch + 1) % N_B, :, cols], preferred_element_type=F32)
         routed = zsum[j, :b_dev]
-        wait_beside(j)
-        recv_wait(zrecv.at[j], zr.at[j, 1])
-        routed = routed + zside[j, :b_dev] + zrecv[j]
+        for dz in range(1, nz):
+            recv_wait(zrecv.at[j, dz - 1], zr.at[j, dz - 1])
+            routed = routed + zrecv[j, dz - 1]
         y_ref[:, cols] = (h1_ref[:, cols].astype(F32) + s + routed).astype(BF16)
 
     for d in range(1, n):
         meta_copy(d).wait_send()
-    for k, z in enumerate(others):
-        u_copy(k, on(z)).wait_send()
-        fwd_copy(z).wait_send()
-    u_copy(nz - 1, dev(mate)).wait_send()
-
-    @pl.loop(0, n_ch)
-    def _(j):
+    for dz in range(1, nz):
+        u_copy(dz - 1, at_z(dz)).wait_send()
+        fwd_copy(dz).wait_send()
+    u_copy(nz - 1, mate).wait_send()
+    for j in range(n_ch):
         p_copy(j).wait_send()
-
-        @pl.when(inner)
-        def _():
-            to_beside(j, 1).wait_send()
-            to_other(j, 0, across).wait_send()
-            to_other(j, 1, far).wait_send()
-
-        @pl.when(jnp.logical_not(inner))
-        def _():
-            to_beside(j, nz - 1).wait_send()
+        for dz in range(1, nz):
+            z_copy(j, dz).wait_send()
 
 
 def moe(n, u, h1, meta, eg, eu, ed, sg, su, sd, cap):
@@ -561,15 +512,14 @@
             pltpu.VMEM((n_ch, half, CW), F32),
             pltpu.VMEM((n_ch, half, CW), F32),
             pltpu.VMEM((n_ch, half, CW), F32),
-            pltpu.VMEM((n_ch, (nz - 1) * b_dev, CW), F32),
-            pltpu.VMEM((n_ch, b_dev, CW), F32),
+            pltpu.VMEM((n_ch, nz - 1, b_dev, CW), F32),
             pltpu.VMEM((b_dev, 2 * inter), BF16),
             dma((3,)), dma((N_A,)), dma((N_B,)),
             dma((n - 1,)), dma((n - 1,)),
-            dma((nz,)), dma((nz + 1,)),
             dma((nz,)), dma((nz,)),
+            dma((nz - 1,)), dma((nz - 1,)),
             dma((n_ch,)), dma((n_ch,)),
-            dma((n_ch, 3)), dma((n_ch, 2)),
+            dma((n_ch, nz - 1)), dma((n_ch, nz - 1)),
         ],
         compiler_params=pltpu.CompilerParams(
             collective_id=0, has_side_effects=True, vmem_limit_bytes=63 << 20),

time: 101 us -> 92.6 us (0.917); the launches traced: 99.4 us -> 92.4 us
  Pallas kernels: 97.2 us -> 90.2 us
    pallas_call x1, Pallas kernels: 81.3 us -> 74.2 us  [moe(): pl.pallas_call(functools.partial(moe_kernel, n, cap), out_shape=jax.Shape...]
where the time goes in v6:
time: 92.6 us; the launch traced here: 92.4 us
  Pallas kernels  90.2 us (97%)
  local copies, waits for them, and re-layouts  1.57 us (2%)
    pallas_call x1, Pallas kernels, moe(): pl.pallas_call(functools.partial(moe_kernel, n, cap), out_shape=jax.Shape...  74.2 us
    pallas_call x1, Pallas kernels, attention(): pl.pallas_call(attn_kernel, out_shape=(row, row, jax.ShapeDtypeStruct((bs...  16.1 us

profile of v6, /device:TPU:0, one launch (start us, length us, event | category | flops | bytes accessed | tf_op | source)
XLA Modules:
  0.0 92.4 jit_solution(18431952819337297681)
XLA Ops:
  0.6 16.1 %attn.1 = (bf16[32,2048]{1,0:T(8,128)(2,1)}, bf16[32,2048]{1,0:T(8,128)(2,1)}, bf16[32,576]{1,0:T(8,128)(2,1)}, f32[16,256]{1,0:T(8,128)}) custom-call(bf16[32,2048]{1,0:T(8,128)(2,1)} %x_in.1, s32[1,32]{1,0:T(1,128)} %bitcast.9, s32[32]{0:T(128)} %lens_in.1, s32[6,32]{1,0:T(8,128)} %bitcast.7, f32[6,32]{1,0:T(8,128)} %bitcast.8, bf16[2048,3072]{1,0:T(8,128)(2,1)} %wq.1, ...), custom_call_target="tpu_custom_call" | custom-call | flops 1149239296 | bytes 36962304 | tf_op jit(solution)/shard_map/attn/pallas_call | solution.py:175
  16.7 74.2 %moe.1 = bf16[32,2048]{1,0:T(8,128)(2,1)} custom-call(bf16[32,2048]{1,0:T(8,128)(2,1)} %get-tuple-element.6.u_in, bf16[32,2048]{1,0:T(8,128)(2,1)} %get-tuple-element.7.h1_in, f32[16,256]{1,0:T(8,128)} %get-tuple-element.8.meta_in, bf16[8,2048,1408]{2,1,0:T(8,128)(2,1)} %eg.1, bf16[8,2048,1408]{2,1,0:T(8,128)(2,1)} %eu.1, bf16[8,1408,2048]{2,1,0:T(8,128)(2,1)} %ed.1, ...), custom_call_target="tpu_custom_call" | custom-call | flops 7751073792 | bytes 173015040 | tf_op jit(solution)/shard_map/moe/pallas_call | solution.py:492
  90.9 1.6 %copy.19 = bf16[32,2048]{1,0:T(8,128)(2,1)} copy(bf16[32,2048]{1,0:T(8,128)(2,1)} %moe.1) | data formatting | bytes 262144

commit v7 on v6

--- a/solution.py
+++ b/solution.py
@@ -13,26 +13,26 @@
 CAP_FACTOR = 2
 N_A = 5
 N_B = 3
-CW = 256
+CW = 512
+GW = 256
+PER = 4
 F32 = jnp.float32
 BF16 = jnp.bfloat16
 
 
 def attn_kernel(x_in, lrow_in, lens_in, ids_in, rw_in, wq, wdkv, wuk, wuv, wo, cache,
                 h1_ref, u_ref, kvn_ref, meta_ref,
-                x_ref, lrow_ref, lens_ref, ids_ref, rw_ref, wq_b, wdkv_b, wuk_b, wuv_b, wo_b, cache_b, q_s, ql_s, qr_s, kv_s, s_s, p_s, ol_s, o_s, sems):
+                x_ref, lrow_ref, lens_ref, ids_ref, rw_ref, wq_b, wdkv_b, wuk_b, wuv_b, wo_b, cache_b, q_a, a_s, q_s, ql_s, qr_s, kv_s, s_s, p_s, ol_s, o_s, sems):
     bsz, hid = x_in.shape
     heads, nope, kvl = wuk.shape
     kvd = wdkv.shape[0]
     rot = kvd - kvl
     l_max = cache.shape[2]
     qkd = nope + rot
-    n_q = 3
-    qc = wq.shape[1] // n_q
+    hh = hid // 2
     n_c = 4
     bc = bsz // n_c
-    n_o = 2
-    oc = hid // n_o
+    oh_dim = wo.shape[0] // 2
     copies = []
 
     def start(src, dst):
@@ -43,12 +43,12 @@
 
     c_x = start(x_in, x_ref)
     c_small = [start(a, b) for a, b in ((lrow_in, lrow_ref), (lens_in, lens_ref), (ids_in, ids_ref), (rw_in, rw_ref))]
-    c_q = [start(wq.at[:, i * qc:(i + 1) * qc], wq_b.at[:, i * qc:(i + 1) * qc]) for i in range(n_q)]
+    c_q = [start(wq.at[i * hh:(i + 1) * hh], wq_b.at[i * hh:(i + 1) * hh]) for i in range(2)]
     c_kv = start(wdkv, wdkv_b)
     c_uk = start(wuk, wuk_b)
     c_c = [start(cache.at[i * bc:(i + 1) * bc], cache_b.at[i * bc:(i + 1) * bc]) for i in range(n_c)]
     c_uv = start(wuv, wuv_b)
-    c_o = [start(wo.at[:, i * oc:(i + 1) * oc], wo_b.at[:, i * oc:(i + 1) * oc]) for i in range(n_o)]
+    c_o = [start(wo.at[i * oh_dim:(i + 1) * oh_dim], wo_b.at[i * oh_dim:(i + 1) * oh_dim]) for i in range(2)]
 
     c_x.wait()
     for c in c_small:
@@ -80,10 +80,10 @@
         return v * lax.rsqrt(jnp.mean(v * v, axis=-1, keepdims=True) + EPS)
 
     xn = norm(x_ref[...].astype(F32)).astype(BF16)
-    for i in range(n_q):
-        c_q[i].wait()
-        q_s[:, i * qc:(i + 1) * qc] = jnp.dot(
-            xn, wq_b[:, i * qc:(i + 1) * qc], preferred_element_type=F32).astype(BF16)
+    c_q[0].wait()
+    q_a[...] = jnp.dot(xn[:, :hh], wq_b[:hh], preferred_element_type=F32)
+    c_q[1].wait()
+    q_s[...] = (q_a[...] + jnp.dot(xn[:, hh:], wq_b[hh:], preferred_element_type=F32)).astype(BF16)
     c_kv.wait()
     kv = lax.dot_general(xn, wdkv_b[...], (((1,), (1,)), ((), ())), preferred_element_type=F32)
     kvn_ref[:, :kvl] = norm(kv[:, :kvl]).astype(BF16)
@@ -150,15 +150,13 @@
         oh = jnp.concatenate(
             [ol_s[g, pl.ds(h, bsz, stride=heads), :] for g in range(kvl // 128)], axis=1).astype(BF16)
         o_s[:, h * vh:(h + 1) * vh] = jnp.dot(oh, wuv_b[h], preferred_element_type=F32).astype(BF16)
-    sq = jnp.zeros((bsz, 1), F32)
-    for i in range(n_o):
-        c_o[i].wait()
-        cols = slice(i * oc, (i + 1) * oc)
-        a = jnp.dot(o_s[...], wo_b[:, cols], preferred_element_type=F32)
-        h1 = (x_ref[:, cols].astype(F32) + a).astype(BF16)
-        h1_ref[:, cols] = h1
-        h1 = h1.astype(F32)
-        sq += jnp.sum(h1 * h1, axis=1, keepdims=True)
+    c_o[0].wait()
+    a_s[...] = jnp.dot(o_s[:, :oh_dim], wo_b[:oh_dim], preferred_element_type=F32)
+    c_o[1].wait()
+    a = a_s[...] + jnp.dot(o_s[:, oh_dim:], wo_b[oh_dim:], preferred_element_type=F32)
+    h1_ref[...] = (x_ref[...].astype(F32) + a).astype(BF16)
+    h1 = h1_ref[...].astype(F32)
+    sq = jnp.sum(h1 * h1, axis=1, keepdims=True)
     u_ref[...] = (h1_ref[...].astype(F32) * lax.rsqrt(sq / hid + EPS)).astype(BF16)
 
 
@@ -184,6 +182,8 @@
             pltpu.VMEM(ids.shape[::-1], jnp.int32),
             pltpu.VMEM(rw.shape[::-1], F32),
         ] + [pltpu.VMEM(w.shape, BF16) for w in weights] + [
+            pltpu.VMEM((bsz, w_q.shape[1]), F32),
+            pltpu.VMEM((bsz, hid), F32),
             pltpu.VMEM((bsz, w_q.shape[1]), BF16),
             pltpu.VMEM((kvl // 128, rows, 128), F32),
             pltpu.VMEM((rows, 128), F32),
@@ -230,11 +230,16 @@
     def a_copy(src, slot):
         return pltpu.make_async_copy(src, wa.at[slot], sem_a.at[slot])
 
-    def start_down(j):
-        slot = lax.rem(j, N_B)
-        for e in range(e_loc):
+    parts = e_loc // PER
+    n_st = n_ch * parts
+
+    def start_down(t):
+        slot = lax.rem(t, N_B)
+        j = t // parts
+        first = lax.rem(t, parts) * PER
+        for e in range(PER):
             pltpu.make_async_copy(
-                ed.at[e, :, pl.ds(pl.multiple_of(j * CW, CW), CW)],
+                ed.at[first + e, :, pl.ds(pl.multiple_of(j * CW, CW), CW)],
                 wb.at[slot, :, pl.ds(e * CW, CW)], sem_b.at[slot]).start()
 
     def wait_a(slot):
@@ -353,8 +358,8 @@
         xr[:, cols] = jnp.dot(disp[...], u_all[:, cols], preferred_element_type=F32).astype(BF16)
 
     def gate_up(x, sa, sb, store):
-        for c0 in range(0, inter, CW):
-            c1 = min(c0 + CW, inter)
+        for c0 in range(0, inter, GW):
+            c1 = min(c0 + GW, inter)
             g = jnp.dot(x, wa[sa, :, c0:c1], preferred_element_type=F32)
             v = jnp.dot(x, wa[sb, :, c0:c1], preferred_element_type=F32)
             store(c0, c1, (jax.nn.silu(g) * v).astype(BF16))
@@ -409,34 +414,38 @@
         for dz in range(1, nz):
             z_copy(j, dz).start()
 
-    @pl.loop(0, n_ch)
-    def _(j):
-        slot = lax.rem(j, N_B)
+    @pl.loop(0, n_st)
+    def _(t):
+        slot = lax.rem(t, N_B)
+        j = t // parts
+        first = lax.rem(t, parts) * PER * cap
         wait_b(slot)
-        for e in range(e_loc):
-            rows[e * cap:(e + 1) * cap] = jnp.dot(
-                act[e * cap:(e + 1) * cap], wb[slot, :, e * CW:(e + 1) * CW],
-                preferred_element_type=F32).astype(BF16)
-
-        @pl.when(j + N_B < n_ch)
+        for e in range(PER):
+            rs = pl.ds(pl.multiple_of(first + e * cap, cap), cap)
+            rows[rs] = jnp.dot(
+                act[rs], wb[slot, :, e * CW:(e + 1) * CW], preferred_element_type=F32).astype(BF16)
+
+        @pl.when(t + N_B < n_st)
         def _():
-            start_down(lax.min(j + N_B, n_ch - 1))
+            start_down(lax.min(t + N_B, n_st - 1))
 
         for h in range(2):
-            i = n_ch + h
-
-            @pl.when(j + N_B == i)
+            i = n_st + h
+
+            @pl.when(t + N_B == i)
             def _():
                 pltpu.make_async_copy(sd.at[pl.ds(h * inter, inter)], wb.at[i % N_B], sem_b.at[i % N_B]).start()
 
-        part = jnp.dot(comb[:, 0:slots], rows[...], preferred_element_type=F32)
-        part += jnp.dot(comb[:, slots:2 * slots], rows[...], preferred_element_type=F32)
-        part += jnp.dot(comb[:, 2 * slots:3 * slots], rows[...], preferred_element_type=F32)
-        pown[j] = part[:half]
-        psend[j] = part[half:]
-        p_copy(j).start()
-
-        @pl.when(j > 0)
+        @pl.when(lax.rem(t, parts) == parts - 1)
+        def _():
+            part = jnp.dot(comb[:, 0:slots], rows[...], preferred_element_type=F32)
+            part += jnp.dot(comb[:, slots:2 * slots], rows[...], preferred_element_type=F32)
+            part += jnp.dot(comb[:, 2 * slots:3 * slots], rows[...], preferred_element_type=F32)
+            pown[j] = part[:half]
+            psend[j] = part[half:]
+            p_copy(j).start()
+
+        @pl.when(jnp.logical_and(lax.rem(t, parts) == 0, t > 0))
         def _():
             pass_on(lax.max(j - 1, 0))
 
@@ -449,16 +458,16 @@
         def store(c0, c1, val):
             sact[:, h * inter + c0:h * inter + c1] = val
 
-        gate_up(u_ref[...], sa, sb, store)
         if h == 0:
             pass_on(n_ch - 1)
+        gate_up(u_ref[...], sa, sb, store)
     for h in range(2):
-        wait_b((n_ch + h) % N_B)
+        wait_b((n_st + h) % N_B)
 
     for j in range(n_ch):
         cols = slice(j * CW, (j + 1) * CW)
-        s = jnp.dot(sact[:, :inter], wb[n_ch % N_B, :, cols], preferred_element_type=F32)
-        s += jnp.dot(sact[:, inter:], wb[(n_ch + 1) % N_B, :, cols], preferred_element_type=F32)
+        s = jnp.dot(sact[:, :inter], wb[n_st % N_B, :, cols], preferred_element_type=F32)
+        s += jnp.dot(sact[:, inter:], wb[(n_st + 1) % N_B, :, cols], preferred_element_type=F32)
         routed = zsum[j, :b_dev]
         for dz in range(1, nz):
             recv_wait(zrecv.at[j, dz - 1], zr.at[j, dz - 1])

time: 92.6 us -> 92.4 us (level)
  no operation moved by 1% of the time
where the time goes in v7:
time: 92.4 us; the launch traced here: 92.3 us
  Pallas kernels  90 us (97%)
  local copies, waits for them, and re-layouts  1.57 us (2%)
    pallas_call x1, Pallas kernels, moe(): pl.pallas_call(functools.partial(moe_kernel, n, cap), out_shape=jax.Shape...  74.2 us
    pallas_call x1, Pallas kernels, attention(): pl.pallas_call(attn_kernel, out_shape=(row, row, jax.ShapeDtypeStruct((bs...  15.9 us

profile of v7, /device:TPU:0, one launch (start us, length us, event | category | flops | bytes accessed | tf_op | source)
XLA Modules:
  0.0 92.3 jit_solution(7606231175889608238)
XLA Ops:
  0.6 15.9 %attn.1 = (bf16[32,2048]{1,0:T(8,128)(2,1)}, bf16[32,2048]{1,0:T(8,128)(2,1)}, bf16[32,576]{1,0:T(8,128)(2,1)}, f32[16,256]{1,0:T(8,128)}) custom-call(bf16[32,2048]{1,0:T(8,128)(2,1)} %x_in.1, s32[1,32]{1,0:T(1,128)} %bitcast.9, s32[32]{0:T(128)} %lens_in.1, s32[6,32]{1,0:T(8,128)} %bitcast.7, f32[6,32]{1,0:T(8,128)} %bitcast.8, bf16[2048,3072]{1,0:T(8,128)(2,1)} %wq.1, ...), custom_call_target="tpu_custom_call" | custom-call | flops 1149239296 | bytes 36962304 | tf_op jit(solution)/shard_map/attn/pallas_call | solution.py:173
  16.5 74.2 %moe.1 = bf16[32,2048]{1,0:T(8,128)(2,1)} custom-call(bf16[32,2048]{1,0:T(8,128)(2,1)} %get-tuple-element.6.u_in, bf16[32,2048]{1,0:T(8,128)(2,1)} %get-tuple-element.7.h1_in, f32[16,256]{1,0:T(8,128)} %get-tuple-element.8.meta_in, bf16[8,2048,1408]{2,1,0:T(8,128)(2,1)} %eg.1, bf16[8,2048,1408]{2,1,0:T(8,128)(2,1)} %eu.1, bf16[8,1408,2048]{2,1,0:T(8,128)(2,1)} %ed.1, ...), custom_call_target="tpu_custom_call" | custom-call | flops 7751073792 | bytes 173015040 | tf_op jit(solution)/shard_map/moe/pallas_call | solution.py:501
  90.7 1.6 %copy.19 = bf16[32,2048]{1,0:T(8,128)(2,1)} copy(bf16[32,2048]{1,0:T(8,128)(2,1)} %moe.1) | data formatting | bytes 262144
